TPU v7x, 256 devices: a 2x2x32 block of a 4x8x32 slice. The times are simulated.
256 devices in a mesh: groups: 4 (over y, x), seq: 32 (over z), batch: 2 (over core).
Axes of the slice: x: 2, y: 2, z: 32, core: 2. Of those that a mesh axis runs over, the one named last changes fastest.
The devices are a block of a 4x8x32 slice.
Arguments:
- prompt_cache: bfloat16 [32, 1024, 8, 256], P(('groups', 'batch'), 'seq'), parts along dimension 0, may hold values from -6 to 6
- prompt_states: float32 [32, 32, 16, 16384], P(('groups', 'batch'), 'seq'), parts along dimension 0, may hold values from -6 to 6
- block_steps: float32 [32, 32, 16384], P(('groups', 'batch'), 'seq'), parts along dimension 0, may hold values from 0.005 to 0.1
- prompt_lengths: int32 [32], P('groups'), parts along dimension 0, may hold values from 170 to 1023
- target_slots: int32 [32], P('groups'), parts along dimension 0, may hold values from 0 to 15, as said below
- cache_lengths: int32 [64], P(('groups', 'batch')), parts along dimension 0, may hold values from 170 to 1023
- resident_cache: bfloat16 [64, 32, 32, 8, 256], P(('groups', 'batch'), None, 'seq'), parts along dimension 0, may hold values from -6 to 6
- token_cache: bfloat16 [64, 8, 256], P(('groups', 'batch')), parts along dimension 0, may hold values from -6 to 6
- queries: bfloat16 [64, 64, 128], P(('groups', 'batch')), parts along dimension 0, may hold values from -6 to 6
- resident_states: float32 [64, 16, 16384], P(('groups', 'batch'), None, 'seq'), parts along dimension 0, may hold values from -6 to 6
- decay_rates: float32 [16, 16384], replicated, may hold values from 0.05 to 10
- step_sizes: float32 [64, 16384], P(('groups', 'batch'), 'seq'), parts along dimension 0, may hold values from 0.01 to 1
- inner_input: bfloat16 [64, 16384], P(('groups', 'batch'), 'seq'), parts along dimension 0, may hold values from -6 to 6
- inner_gate: bfloat16 [64, 16384], P(('groups', 'batch'), 'seq'), parts along dimension 0, may hold values from -6 to 6
- state_input: float32 [64, 16], P(('groups', 'batch')), parts along dimension 0, may hold values from -6 to 6
- state_readout: float32 [64, 16], P(('groups', 'batch')), parts along dimension 0, may hold values from -6 to 6
- skip_gain: float32 [16384], P('seq'), may hold values from 0.5 to 1.5
Outputs:
- merged_cache: bfloat16 [64, 32, 32, 8, 256], P(('groups', 'batch'), None, 'seq'), parts along dimension 0
- attention: bfloat16 [64, 64, 128], P(('groups', 'batch'), 'seq'), parts along dimension 0
- next_states: float32 [64, 16, 16384], P(('groups', 'batch'), None, 'seq'), parts along dimension 0
- mamba_output: bfloat16 [64, 16384], P(('groups', 'batch'), 'seq'), parts along dimension 0
There are 4 independent parts, one for each index of `groups`. A program takes and returns all parts, laid end to end along the dimension named above; an argument that names none is the same for every part. Nothing has to cross between parts.
Inputs may be any that keep to these rules, and one draw needn't show every extreme that they name: `target_slots`: 8 distinct slots.
All inputs are finite; a program needn't handle non-finite values.
Results may differ from a plain program's by a relative error of at most 0.0019.
Values may be sent and summed in bfloat16 or wider, within the bound.
A program may use at most 320 MiB of HBM per device.

v0:
```python
import math

import jax
import jax.numpy as jnp
from jax import lax
from jax.sharding import PartitionSpec as P


def carried_in(shard, axis, combine, identity):
    count, position = (lax.axis_size(axis), lax.axis_index(axis))
    everything = lax.all_gather(shard, axis)
    start = jnp.broadcast_to(jnp.asarray(identity, shard.dtype), shard.shape)

    def step(k, before):
        at = count - 1 - k
        reached = at > position
        new = combine(before, everything[at])
        return jnp.where(reached, new, before)

    return lax.fori_loop(0, count, step, start)


def sent_to_all(shard, axis):
    count = lax.axis_size(axis)
    return lax.all_to_all(
        jnp.broadcast_to(shard[None], (count, *shard.shape)), axis, 0, 0, tiled=True
    )


def joined_along(pieces, dim):
    pieces = jnp.moveaxis(pieces, 0, dim)
    lengths = pieces.shape
    return pieces.reshape(*lengths[:dim], lengths[dim] * lengths[dim + 1], *lengths[dim + 2 :])


def gather_directly(shard, axis, dim):
    pieces = sent_to_all(shard, axis)
    return joined_along(pieces, dim)


def add_terms(earlier, latter):
    return earlier + latter


def to_cyclic(blocks, seq_count):
    count, length, heads, width = blocks.shape
    return blocks.reshape(count, length // seq_count, seq_count, heads, width)


def block_usable(lengths, seq_index, block_len):
    return (seq_index * block_len < lengths).astype(jnp.float32)


def decay_term(states, behind, usable, rates):
    return usable[:, None, None] * jnp.exp(-rates[None] * behind[:, None, :]) * states


def local(
    prompt_cache,
    prompt_states,
    block_steps,
    prompt_lengths,
    target_slots,
    cache_lengths,
    resident_cache,
    token_cache,
    queries,
    resident_states,
    decay_rates,
    step_sizes,
    inner_input,
    inner_gate,
    state_input,
    state_readout,
    skip_gain,
):
    seq_count = lax.axis_size("seq")
    seq_index = lax.axis_index("seq")
    batch_index = lax.axis_index("batch")
    local_prompts, block_len, kv_heads, kv_width = prompt_cache.shape
    head_dim = kv_width // 2
    requests = resident_cache.shape[0]
    channels = decay_rates.shape[1]
    local_channels = channels // seq_count
    own_lengths = lax.dynamic_slice_in_dim(
        prompt_lengths, batch_index * local_prompts, local_prompts
    )
    usable = block_usable(own_lengths, seq_index, block_len)
    moved = lax.all_to_all(
        to_cyclic(prompt_cache, seq_count), "seq", split_axis=2, concat_axis=1, tiled=True
    )
    step_terms = block_steps[:, 0, :] * usable[:, None]
    behind = carried_in(step_terms, "seq", add_terms, jnp.zeros_like(step_terms))
    handed_share = lax.psum_scatter(
        decay_term(prompt_states[:, 0], behind, usable, decay_rates),
        "seq",
        scatter_dimension=2,
        tiled=True,
    )
    arrived = lax.all_gather(moved[:, :, 0], "batch", axis=0, tiled=True)
    handed = gather_directly(handed_share, "batch", 0)
    prompt_count = arrived.shape[0]
    slot_ids = batch_index * requests + jnp.arange(requests, dtype=jnp.int32)
    matches = target_slots[None, :] == slot_ids[:, None]
    fresh = jnp.any(matches, axis=1)
    chosen_len = jnp.sum(jnp.where(matches, prompt_lengths[None, :], 0), axis=1)
    lengths = jnp.where(fresh, chosen_len, cache_lengths)
    picked = jnp.dot(
        matches.astype(jnp.bfloat16),
        arrived.reshape(prompt_count, -1),
        preferred_element_type=jnp.float32,
    )
    picked = picked.astype(jnp.bfloat16).reshape(requests, block_len, kv_heads, kv_width)
    position = jnp.arange(block_len, dtype=jnp.int32) * seq_count + seq_index
    merged = jnp.where(fresh[:, None, None, None], picked, resident_cache[:, :, 0])
    merged = jnp.where(
        (position[None, :] < lengths[:, None])[:, :, None, None],
        merged,
        jnp.zeros((), jnp.bfloat16),
    )
    merged = jnp.where(
        (position[None, :] == lengths[:, None])[:, :, None, None], token_cache[:, None], merged
    )
    heads = queries.shape[1]
    group = heads // kv_heads
    grouped = queries.reshape(requests, kv_heads, group, head_dim)
    scores = jnp.einsum(
        "rgqd,rtgd->rgqt", grouped, merged[..., :head_dim], preferred_element_type=jnp.float32
    ) * (1.0 / math.sqrt(head_dim))
    seen = (position[None, :] <= lengths[:, None])[:, None, None, :]
    masked = jnp.where(seen, scores, -1e30)
    highest = jnp.max(masked, axis=3)
    weights = jnp.where(seen, jnp.exp(masked - highest[..., None]), 0.0)
    denominator = jnp.sum(weights, axis=3)
    summed = jnp.einsum(
        "rgqt,rtgd->rgqd",
        weights.astype(jnp.bfloat16),
        merged[..., head_dim:],
        preferred_element_type=jnp.float32,
    )
    highest = highest.reshape(requests, heads)
    denominator = denominator.reshape(requests, heads)
    summed = summed.reshape(requests, heads, head_dim)
    peer_top, peer_total, peer_sum = (
        lax.all_to_all(highest[:, None], "seq", split_axis=2, concat_axis=1, tiled=True),
        lax.all_to_all(denominator[:, None], "seq", split_axis=2, concat_axis=1, tiled=True),
        lax.all_to_all(summed[:, None], "seq", split_axis=2, concat_axis=1, tiled=True),
    )
    common_top = jnp.max(peer_top, axis=1)
    factor = jnp.exp(peer_top - common_top[:, None])
    owner_total = jnp.sum(peer_total * factor, axis=1)
    owner_sum = jnp.sum(peer_sum * factor[..., None], axis=1)
    attention = (owner_sum / owner_total[..., None]).astype(jnp.bfloat16)
    rates_here = lax.dynamic_slice_in_dim(
        decay_rates, seq_index * local_channels, local_channels, 1
    )
    chosen_state = jnp.einsum(
        "rp,pnc->rnc", matches.astype(jnp.float32), handed, precision=lax.Precision.HIGHEST
    )
    start = jnp.where(fresh[:, None, None], chosen_state, resident_states)
    inner = inner_input.astype(jnp.float32)
    next_states = (
        jnp.exp(-rates_here[None] * step_sizes[:, None, :]) * start
        + (step_sizes * inner)[:, None, :] * state_input[:, :, None]
    )
    readout = jnp.sum(state_readout[:, :, None] * next_states, axis=1) + skip_gain[None, :] * inner
    mamba_output = (readout * jax.nn.silu(inner_gate.astype(jnp.float32))).astype(jnp.bfloat16)
    return (merged[:, :, None], attention, next_states, mamba_output)


def solution(mesh):
    return jax.shard_map(
        local,
        mesh=mesh,
        in_specs=(
            P(("groups", "batch"), "seq", None, None),
            P(("groups", "batch"), "seq", None, None),
            P(("groups", "batch"), "seq", None),
            P("groups"),
            P("groups"),
            P(("groups", "batch")),
            P(("groups", "batch"), None, "seq", None, None),
            P(("groups", "batch"), None, None),
            P(("groups", "batch"), None, None),
            P(("groups", "batch"), None, "seq"),
            P(),
            P(("groups", "batch"), "seq"),
            P(("groups", "batch"), "seq"),
            P(("groups", "batch"), "seq"),
            P(("groups", "batch"), None),
            P(("groups", "batch"), None),
            P("seq"),
        ),
        out_specs=(
            P(("groups", "batch"), None, "seq", None, None),
            P(("groups", "batch"), "seq", None),
            P(("groups", "batch"), None, "seq"),
            P(("groups", "batch"), "seq"),
        ),
        check_vma=False,
    )
```

profile of v0, /device:TPU:37, one launch (start us, length us, event | category | flops | bytes accessed | tf_op | source)
XLA Modules:
  0.0 421.0 jit_solution(6203049172755790283)
XLA Ops:
  8.0 1.8 bitcast_multiply_fusion.1
  9.9 1.9 copy.82
  11.8 33.2 %all-to-all-start = ((bf16[4,1,32,8,256]{4,3,0,1,2:T(8,128)(2,1)}), bf16[4,1,32,8,256]{4,3,0,1,2:T(8,128)(2,1)S(1)}, u32[]{:S(2)}, u32[]{:S(2)}) async-start(bf16[4,1,32,8,256]{4,3,0,1,2:T(8,128)(2,1)} %bitcast.42), calls=%async_computation | async-start | bytes 1048576 | tf_op jit(solution)/shard_map/all_to_all | solution.py:89
  45.1 1.4 neg.13
  46.5 67.7 %all-to-all-done = bf16[4,1,32,8,256]{4,3,0,1,2:T(8,128)(2,1)S(1)} async-done(((bf16[4,1,32,8,256]{4,3,0,1,2:T(8,128)(2,1)}), bf16[4,1,32,8,256]{4,3,0,1,2:T(8,128)(2,1)S(1)}, u32[]{:S(2)}, u32[]{:S(2)}) %all-to-all-start) | async-done | bytes 524320 | tf_op jit(solution)/shard_map/all_to_all | solution.py:89
  115.2 79.8 %all-gather.4.cloned.1.call-done = f32[32,4,16384]{2,1,0:T(4,128)} async-done(((f32[1,4,16384]{2,1,0:T(4,128)}), f32[32,4,16384]{2,1,0:T(4,128)}) %all-gather.4.cloned.1.call-update) | async-done | bytes 8388624 | tf_op jit(solution)/shard_map/all_gather | solution.py:11
  195.0 42.3 %while.16 = (s32[]{:T(128)}, f32[4,16384]{1,0:T(4,128)S(1)}, s32[]{:T(128)}, f32[32,4,16384]{2,1,0:T(4,128)}, s32[]{:T(128)}, /*index=5*/s32[]{:T(128)}, s32[]{:T(128)}, s32[]{:T(128)}) while((s32[]{:T(128)}, f32[4,16384]{1,0:T(4,128)S(1)}, s32[]{:T(128)}, f32[32,4,16384]{2,1,0:T(4,128)}, s32[]{:T(128)}, /*index=5*/s32[]{:T(128)}, ...), condition=%wide.region_8.9_spmd.clone, body=%wide.region_7.8_spmd.clone.sunk | while | flops 196616 | bytes 786595 | solution.py:20
  196.4 1.3 add_select_fusion.2
  197.7 1.3 add_select_fusion.2
  199.0 1.3 add_select_fusion.2
  200.3 1.3 add_select_fusion.2
  201.6 1.3 add_select_fusion.2
  204.3 1.3 add_select_fusion.2
  208.2 1.3 add_select_fusion.2
  225.4 1.3 add_select_fusion.2
  229.4 1.3 add_select_fusion.2
  230.7 1.3 add_select_fusion.2
  236.0 1.3 add_select_fusion.2
  237.3 4.9 %bitcast_multiply_fusion = f32[4,16,16384]{2,1,0:T(8,128)} fusion(f32[4,1,16,16384]{3,2,1,0:T(8,128)} %param.20, f32[4,16384]{1,0:T(4,128)S(1)} %get-tuple-element.114, f32[16,16384]{1,0:T(8,128)S(1)} %neg.13, f32[4]{0:T(128)S(1)} %compare_convert_fusion), kind=kLoop, calls=%fused_computation.2 | loop fusion | flops 3145728 | bytes 9699344 | tf_op jit(solution)/shard_map/mul | solution.py:55
  243.9 1.8 copy.71
  246.2 1.4 fusion.5
  249.7 1.4 copy.69
  251.1 13.5 %all-to-all-start.3 = ((f32[8,1,64]{0,1,2:T(1,128)}), f32[8,1,64]{0,1,2:T(1,128)}, u32[]{:S(2)}, u32[]{:S(2)}) async-start(f32[8,1,64]{0,1,2:T(1,128)} %bitcast.51), calls=%async_computation.3 | async-start | bytes 65536 | tf_op jit(solution)/shard_map/all_to_all | solution.py:146
  264.6 1.4 copy.60
  266.0 20.0 %all-to-all-done.3 = f32[8,1,64]{0,1,2:T(1,128)} async-done(((f32[8,1,64]{0,1,2:T(1,128)}), f32[8,1,64]{0,1,2:T(1,128)}, u32[]{:S(2)}, u32[]{:S(2)}) %all-to-all-start.3) | async-done | bytes 2080 | tf_op jit(solution)/shard_map/all_to_all | solution.py:146
  286.0 5.4 %all-to-all-start.2 = ((f32[8,1,64]{0,1,2:T(1,128)}), f32[8,1,64]{0,1,2:T(1,128)}, u32[]{:S(2)}, u32[]{:S(2)}) async-start(f32[8,1,64]{0,1,2:T(1,128)} %bitcast.50), calls=%async_computation.2 | async-start | bytes 65536 | tf_op jit(solution)/shard_map/all_to_all | solution.py:145
  293.4 19.3 %all-to-all-done.2 = f32[8,1,64]{0,1,2:T(1,128)} async-done(((f32[8,1,64]{0,1,2:T(1,128)}), f32[8,1,64]{0,1,2:T(1,128)}, u32[]{:S(2)}, u32[]{:S(2)}) %all-to-all-start.2) | async-done | bytes 2080 | tf_op jit(solution)/shard_map/all_to_all | solution.py:145
  312.7 4.8 %all-to-all-start.1 = ((f32[8,1,64,128]{3,0,1,2:T(8,128)}), f32[8,1,64,128]{3,0,1,2:T(8,128)S(1)}, u32[]{:S(2)}, u32[]{:S(2)}) async-start(f32[8,1,64,128]{3,0,1,2:T(8,128)} %copy.59), calls=%async_computation.1 | async-start | bytes 524288 | tf_op jit(solution)/shard_map/all_to_all | solution.py:147
  320.5 2.3 fusion.7
  324.4 26.6 %all-to-all-done.1 = f32[8,1,64,128]{3,0,1,2:T(8,128)S(1)} async-done(((f32[8,1,64,128]{3,0,1,2:T(8,128)}), f32[8,1,64,128]{3,0,1,2:T(8,128)S(1)}, u32[]{:S(2)}, u32[]{:S(2)}) %all-to-all-start.1) | async-done | bytes 262176 | tf_op jit(solution)/shard_map/all_to_all | solution.py:147
  351.8 38.6 %reduce-scatter.2.cloned.1.call-done = f32[4,16,512]{2,1,0:T(8,128)} async-done(((f32[4,16,16384]{2,1,0:T(8,128)}), f32[4,16,512]{2,1,0:T(8,128)}) %reduce-scatter.2.cloned.1.call-update) | async-done | bytes 131088 | tf_op jit(solution)/shard_map/reduce_scatter | solution.py:94
  391.5 20.9 %all_to_all.50 = f32[2,4,16,512]{3,1,2,0:T(4,128)S(1)} all-to-all(f32[2,4,16,512]{3,1,2,0:T(4,128)S(1)} %broadcast_in_dim.143), channel_id=1, replica_groups=mesh['groups'=4,'seq'=32,'batch'=2] {'batch'}, dimensions={0} | all-to-all | bytes 524288 | tf_op jit(solution)/shard_map/all_to_all | solution.py:25
  (98 shorter events, 43.9 us)
Async XLA Ops:
  7.2 240.5 %copy-start = (bf16[8,64,128]{2,1,0:T(8,128)(2,1)S(1)}, bf16[8,64,128]{2,1,0:T(8,128)(2,1)}, u32[]{:S(2)}) copy-start(bf16[8,64,128]{2,1,0:T(8,128)(2,1)} %param.27) | copy-start | bytes 393220
  7.2 187.8 %all-gather.4.cloned.1.call-start = ((), (), s32[]{:S(2)}) async-start(), calls=%async_computation.6 | async-start | bytes 8650752 | tf_op jit(solution)/shard_map/all_gather | solution.py:11
  11.8 102.4 %all-to-all-start = ((bf16[4,1,32,8,256]{4,3,0,1,2:T(8,128)(2,1)}), bf16[4,1,32,8,256]{4,3,0,1,2:T(8,128)(2,1)S(1)}, u32[]{:S(2)}, u32[]{:S(2)}) async-start(bf16[4,1,32,8,256]{4,3,0,1,2:T(8,128)(2,1)} %bitcast.42), calls=%async_computation | async-start | bytes 1048576 | tf_op jit(solution)/shard_map/all_to_all | solution.py:89
  45.0 198.9 %all-gather.6.cloned.1.call-start = ((), (), s32[]{:S(2)}) async-start(), calls=%async_computation.8 | async-start | bytes 1572864 | tf_op jit(solution)/shard_map/all_gather | solution.py:100
  115.1 275.3 %reduce-scatter.2.cloned.1.call-start = ((), (), s32[]{:S(2)}) async-start(), calls=%async_computation.7 | async-start | bytes 4325376 | tf_op jit(solution)/shard_map/reduce_scatter | solution.py:94
  242.2 0.7 copy-start.13
  242.2 0.8 copy-start.17
  242.2 1.0 copy-start.19
  242.2 4.0 copy-start.1
  242.2 4.0 copy-start.4
  242.8 4.8 %copy-start.15 = (s32[8]{0:T(128)}, s32[8]{0:T(128)S(1)}, u32[]{:S(2)}) copy-start(s32[8]{0:T(128)S(1)} %iota_add_fusion) | copy-start | bytes 100
  243.0 4.6 %copy-start.10 = (pred[8]{0:T(512)(128)(4,1)}, pred[8]{0:T(512)(128)(4,1)S(1)}, u32[]{:S(2)}) copy-start(pred[8]{0:T(512)(128)(4,1)S(1)} %compare_reduce_fusion) | copy-start | bytes 28
  243.9 3.8 copy-start.7
  243.9 3.8 copy-start.8
  243.9 3.8 copy-start.9
  245.7 74.1 %copy-start.5 = (f32[8,512]{1,0:T(8,128)S(1)}, f32[8,512]{1,0:T(8,128)}, u32[]{:S(2)}) copy-start(f32[8,512]{1,0:T(8,128)} %param.30) | copy-start | bytes 49156
  248.1 0.6 copy-start.2
  251.1 34.9 %all-to-all-start.3 = ((f32[8,1,64]{0,1,2:T(1,128)}), f32[8,1,64]{0,1,2:T(1,128)}, u32[]{:S(2)}, u32[]{:S(2)}) async-start(f32[8,1,64]{0,1,2:T(1,128)} %bitcast.51), calls=%async_computation.3 | async-start | bytes 65536 | tf_op jit(solution)/shard_map/all_to_all | solution.py:146
  286.0 26.7 %all-to-all-start.2 = ((f32[8,1,64]{0,1,2:T(1,128)}), f32[8,1,64]{0,1,2:T(1,128)}, u32[]{:S(2)}, u32[]{:S(2)}) async-start(f32[8,1,64]{0,1,2:T(1,128)} %bitcast.50), calls=%async_computation.2 | async-start | bytes 65536 | tf_op jit(solution)/shard_map/all_to_all | solution.py:145
  292.4 120.1 %copy-start.3 = (f32[8,16,512]{2,1,0:T(8,128)S(1)}, f32[8,16,512]{2,1,0:T(8,128)}, u32[]{:S(2)}) copy-start(f32[8,16,512]{2,1,0:T(8,128)} %param.28) | copy-start | bytes 786436
  292.4 120.1 %copy-start.11 = (pred[8]{0:T(512)(128)(4,1)S(1)}, pred[8]{0:T(512)(128)(4,1)}, u32[]{:S(2)}) copy-start(pred[8]{0:T(512)(128)(4,1)} %copy-done.10) | copy-start | bytes 28
  292.5 120.1 %copy-start.14 = (s32[8]{0:T(128)S(1)}, s32[8]{0:T(128)}, u32[]{:S(2)}) copy-start(s32[8]{0:T(128)} %param.23) | copy-start | bytes 100
  292.5 120.1 %copy-start.16 = (s32[8]{0:T(128)S(1)}, s32[8]{0:T(128)}, u32[]{:S(2)}) copy-start(s32[8]{0:T(128)} %copy-done.15) | copy-start | bytes 100
  292.5 121.4 %copy-start.6 = (bf16[8,512]{1,0:T(8,128)(2,1)S(1)}, bf16[8,512]{1,0:T(8,128)(2,1)}, u32[]{:S(2)}) copy-start(bf16[8,512]{1,0:T(8,128)(2,1)} %param.31) | copy-start | bytes 24580
  292.5 121.4 %copy-start.12 = (bf16[8,512]{1,0:T(8,128)(2,1)S(1)}, bf16[8,512]{1,0:T(8,128)(2,1)}, u32[]{:S(2)}) copy-start(bf16[8,512]{1,0:T(8,128)(2,1)} %param.32) | copy-start | bytes 24580
  292.5 121.4 %copy-start.18 = (f32[512]{0:T(512)S(1)}, f32[512]{0:T(512)}, u32[]{:S(2)}) copy-start(f32[512]{0:T(512)} %param.35) | copy-start | bytes 6148
  312.7 38.3 %all-to-all-start.1 = ((f32[8,1,64,128]{3,0,1,2:T(8,128)}), f32[8,1,64,128]{3,0,1,2:T(8,128)S(1)}, u32[]{:S(2)}, u32[]{:S(2)}) async-start(f32[8,1,64,128]{3,0,1,2:T(8,128)} %copy.59), calls=%async_computation.1 | async-start | bytes 524288 | tf_op jit(solution)/shard_map/all_to_all | solution.py:147
Sparse Core Ops, SparseCore 0:
  10.4 184.5 all-gather.3
  197.4 36.6 all-gather.5
  242.4 147.9 reduce-scatter.1
where the time goes:
time: 424 us; the launch traced here: 421 us
  waiting for transfers between devices  252 us (59%)
  other arithmetic  60.1 us (14%)
  starting transfers between devices  57 us (13%)
  blocking collectives  20.9 us (5%)
  between operations  14.1 us (3%)
  local copies, waits for them, and re-layouts  13.7 us (3%)
    all_gather x1, waiting for transfers between devices, carried_in(): everything = lax.all_gather(shard, axis)  79.8 us
    all_to_all x1, waiting for transfers between devices, local(): lax.all_to_all(to_cyclic(prompt_cache, seq_count), 'seq', split_axis=2, c...  67.7 us
    select_n x32, other arithmetic, step(): return jnp.where(reached, new, before)  41.8 us
    reduce_scatter x1, waiting for transfers between devices, local(): lax.psum_scatter(decay_term(prompt_states[:, 0], behind, usable, decay_ra...  38.6 us
    all_to_all x1, starting transfers between devices, local(): lax.all_to_all(to_cyclic(prompt_cache, seq_count), 'seq', split_axis=2, c...  33.2 us
    all_to_all x1, waiting for transfers between devices, local(): lax.all_to_all(summed[:, None], 'seq', split_axis=2, concat_axis=1, tiled...  26.6 us
    all_to_all x1, blocking collectives, sent_to_all(): lax.all_to_all(jnp.broadcast_to(shard[None], (count, *shard.shape)), axis...  20.9 us
    all_to_all x1, waiting for transfers between devices, local(): lax.all_to_all(denominator[:, None], 'seq', split_axis=2, concat_axis=1,...  20 us
  transfers between devices with their start and end apart: 7, of which 6 were waited for; matrix products, arithmetic and copies ran while one was open for 16% of the time, Pallas kernels for 0%

commit v1 on v0

v1 whole, which is shorter than its diff:
```python
import functools
import math

import jax
import jax.numpy as jnp
from jax import lax
from jax.experimental import pallas as pl
from jax.experimental.pallas import tpu as pltpu
from jax.sharding import PartitionSpec as P

MESH = pl.DeviceIdType.MESH
STEPS_BEFORE_ATTENTION = 5


def kernel(
    n,
    early,
    plen_ref,
    target_ref,
    clen_ref,
    cache_ref,
    steps_ref,
    states_hbm,
    rates,
    resident,
    token_ref,
    query_ref,
    res_state_ref,
    step_size_ref,
    inner_ref,
    gate_ref,
    sin_ref,
    sout_ref,
    skip_ref,
    merged,
    att_ref,
    next_ref,
    mamba_ref,
    states,
    msteps,
    arrived,
    t_up,
    t_dn,
    h_up,
    h_dn,
    r_up,
    r_dn,
    s_up,
    s_dn,
    part_sum,
    part_ml,
    handed,
    load_sem,
    cache_send,
    cache_recv,
    pair_send,
    pair_recv,
    t_send,
    t_recv,
    h_send,
    h_recv,
    r_send,
    r_recv,
    s_send,
    s_recv,
):
    h = n // 2
    me = lax.axis_index("seq")
    core = lax.axis_index("batch")
    up = lax.rem(me + 1, n)
    down = lax.rem(me + n - 1, n)
    prompts, block_len, kv_heads, kv_width = cache_ref.shape
    state = states.shape[1]
    share = handed.shape[3]
    slots, heads, head_dim = query_ref.shape
    rows = block_len * kv_heads
    own_heads = heads // n
    group = heads // kv_heads

    barrier = pltpu.get_barrier_semaphore()

    def greet(k, carry):
        pl.semaphore_signal(
            barrier, inc=1, device_id={"seq": lax.rem(me + k, n)}, device_id_type=MESH
        )
        return carry

    lax.fori_loop(1, n, greet, 0)
    pl.semaphore_signal(barrier, inc=1, device_id={"batch": 1 - core}, device_id_type=MESH)

    load = pltpu.make_async_copy(states_hbm, states, load_sem)
    load.start()

    usable = []
    for p in range(prompts):
        reached = me * block_len < plen_ref[core * prompts + p]
        usable.append(jnp.where(reached, 1.0, 0.0).astype(jnp.float32))
        msteps[p : p + 1, :] = steps_ref[p : p + 1, :] * usable[p]

    def columns(o):
        return pl.ds(pl.multiple_of(o * share, share), share)

    def remote(src, dst, send, recv, where):
        return pltpu.make_async_remote_copy(
            src_ref=src,
            dst_ref=dst,
            send_sem=send,
            recv_sem=recv,
            device_id=where,
            device_id_type=MESH,
        )

    def hop(buf, k, send, recv, to):
        return remote(buf.at[k], buf.at[k + 1], send, recv.at[k + 1], {"seq": to})

    def arrival(buf, k, send, recv, to):
        return remote(buf.at[k], buf.at[k], send, recv.at[k], {"seq": to})

    for p in range(prompts):
        arrived[p, me] = cache_ref[p, me]

    pl.semaphore_wait(barrier, n)

    def add_steps(s):
        o = lax.rem(s + n - h, n)
        mine = msteps[:, columns(o)]
        high = jnp.where(me > s, 1.0, 0.0).astype(jnp.float32)
        return high * mine, (1.0 - high) * mine

    def send_cache(k):
        to = lax.rem(me + k, n)
        remote(
            cache_ref.at[:, to], arrived.at[pl.ds(0, prompts), me], cache_send, cache_recv, {"seq": to}
        ).start()

    def first_steps(buf, s):
        above, below = add_steps(s)
        buf[0, 0:prompts, :] = above
        buf[0, prompts : 2 * prompts, :] = below

    def more_steps(buf, k, s):
        above, below = add_steps(s)
        buf[k, 0:prompts, :] += above
        buf[k, prompts : 2 * prompts, :] += below

    first_steps(t_up, lax.rem(me + h - 1, n))
    first_steps(t_dn, lax.rem(me + n - h, n))
    hop(t_up, 0, t_send.at[0], t_recv.at[0], up).start()
    hop(t_dn, 0, t_send.at[1], t_recv.at[1], down).start()
    send_cache(1)
    send_cache(n - 1)

    def step_ring(k, carry):
        arrival(t_up, k, t_send.at[0], t_recv.at[0], up).wait_recv()
        more_steps(t_up, k, lax.rem(me + h - 1 - k, n))

        @pl.when(k < h - 1)
        def _():
            hop(t_up, k, t_send.at[0], t_recv.at[0], up).start()

        arrival(t_dn, k, t_send.at[1], t_recv.at[1], down).wait_recv()
        more_steps(t_dn, k, lax.rem(me + n - h + k, n))
        hop(t_dn, k, t_send.at[1], t_recv.at[1], down).start()
        send_cache(k + 1)

        @pl.when(k < h - 1)
        def _():
            send_cache(n - 1 - k)

        return carry

    lax.fori_loop(1, h, step_ring, 0)
    arrival(t_dn, h, t_send.at[1], t_recv.at[1], down).wait_recv()
    later = t_up[h - 1, 0:prompts, :] + t_dn[h, 0:prompts, :]
    everything = (
        later + t_up[h - 1, prompts : 2 * prompts, :] + t_dn[h, prompts : 2 * prompts, :]
    )

    load.wait()

    def term(p, o, behind):
        return (
            usable[p]
            * jnp.exp(-rates[:, columns(o)] * behind)
            * states[p, :, columns(o)]
        )

    start = lax.rem(me + n - h, n)
    h_up[0, 0:prompts, :] = later
    h_up[0, prompts : 2 * prompts, :] = everything
    hop(h_up, 0, h_send.at[0], h_recv.at[0], up).start()
    h_dn[0, 0:prompts, :] = later + msteps[:, columns(start)]
    h_dn[0, prompts : 2 * prompts, :] = everything
    hop(h_dn, 0, h_send.at[1], h_recv.at[1], down).start()

    def send_sum(way, buf, k, p, to):
        remote(
            buf.at[k, p], buf.at[k + 1, p], r_send.at[way], r_recv.at[way, k + 1, p], {"seq": to}
        ).start()

    def wait_sum(way, buf, k, p, to):
        remote(
            buf.at[k, p], buf.at[k, p], r_send.at[way], r_recv.at[way, k, p], {"seq": to}
        ).wait_recv()

    for p in range(prompts):
        r_dn[0, p] = term(p, start, later[p : p + 1])
        send_sum(1, r_dn, 0, p, down)

    def header_up(k, o):
        arrival(h_up, k, h_send.at[0], h_recv.at[0], up).wait_recv()
        before = jnp.where(me == 0, h_up[k, prompts : 2 * prompts, :], h_up[k, 0:prompts, :])
        return before - msteps[:, columns(o)]

    def state_step(k, first):
        o_up = lax.rem(me + 2 * n - h - k, n)
        o_dn = lax.rem(me + n - h + k, n)
        behind_up = header_up(k, o_up)
        h_up[k, 0:prompts, :] = behind_up
        hop(h_up, k, h_send.at[0], h_recv.at[0], up).start()
        arrival(h_dn, k, h_send.at[1], h_recv.at[1], down).wait_recv()
        behind_dn = jnp.where(me == n - 1, 0.0, h_dn[k, 0:prompts, :])
        h_dn[k, 0:prompts, :] = behind_dn + msteps[:, columns(o_dn)]

        @pl.when(k < h - 1)
        def _():
            hop(h_dn, k, h_send.at[1], h_recv.at[1], down).start()

        for p in range(prompts):
            up_term = term(p, o_up, behind_up[p : p + 1])
            if first:
                r_up[k, p] = up_term
            else:
                wait_sum(0, r_up, k, p, up)
                r_up[k, p] += up_term
            send_sum(0, r_up, k, p, up)
            dn_term = term(p, o_dn, behind_dn[p : p + 1])
            wait_sum(1, r_dn, k, p, down)
            r_dn[k, p] += dn_term
            send_sum(1, r_dn, k, p, down)

    state_step(1, True)
    lax.fori_loop(2, early, lambda k, c: (state_step(k, False), c)[1], 0)

    remote(
        cache_ref.at[:, pl.ds(0, n - 1)],
        arrived.at[pl.ds(0, prompts), pl.ds(0, n - 1)],
        cache_send,
        cache_recv,
        {"seq": up},
    ).wait()
    cache_pair = remote(
        arrived.at[pl.ds(0, prompts)],
        arrived.at[pl.ds(prompts, prompts)],
        pair_send.at[0],
        pair_recv.at[0],
        {"batch": 1 - core},
    )
    cache_pair.start()
    cache_pair.wait()

    def slot_facts(r):
        slot = core * slots + r
        fresh, length, place = jnp.int32(0), clen_ref[r], jnp.int32(0)
        for q in range(2 * prompts):
            index = lax.rem(core * prompts + q, 2 * prompts)
            hit = target_ref[index] == slot
            fresh = jnp.where(hit, 1, fresh)
            length = jnp.where(hit, plen_ref[index], length)
            place = jnp.where(hit, q, place)
        return fresh == 1, length, place

    def attend(r, carry):
        fresh, length, place = slot_facts(r)
        chosen = jnp.where(
            fresh, arrived[place].astype(jnp.float32), resident[r].astype(jnp.float32)
        )
        position = lax.broadcasted_iota(jnp.int32, chosen.shape, 0) * n + me
        chosen = jnp.where(position < length, chosen, 0.0)
        token = jnp.broadcast_to(token_ref[r].astype(jnp.float32)[None], chosen.shape)
        chosen = jnp.where(position == length, token, chosen)
        merged[r] = chosen.astype(jnp.bfloat16)
        flat = chosen.reshape(rows, kv_width).astype(jnp.bfloat16)
        score = lax.dot_general(
            query_ref[r],
            flat[:, :head_dim],
            (((1,), (1,)), ((), ())),
            preferred_element_type=jnp.float32,
        ) * (1.0 / math.sqrt(head_dim))
        column = lax.broadcasted_iota(jnp.int32, score.shape, 1)
        row = lax.broadcasted_iota(jnp.int32, score.shape, 0)
        seen = (lax.rem(column, kv_heads) == lax.div(row, group)) & (
            lax.div(column, kv_heads) * n + me <= length
        )
        score = jnp.where(seen, score, -1e30)
        top = jnp.max(score, axis=1, keepdims=True)
        weight = jnp.where(seen, jnp.exp(score - top), 0.0)
        total = jnp.sum(weight, axis=1, keepdims=True)
        summed = jnp.dot(
            weight.astype(jnp.bfloat16), flat[:, head_dim:], preferred_element_type=jnp.float32
        )
        at = pl.ds(pl.multiple_of(r * heads, heads), heads)
        part_sum[at, :] = summed
        lane = lax.broadcasted_iota(jnp.int32, summed.shape, 1)
        part_ml[at, :] = jnp.where(lane < head_dim // 2, top, total)
        return carry

    lax.fori_loop(0, slots, attend, 0)

    count = own_heads * slots
    half = head_dim // 2

    def own_part(o):
        sums = [
            part_sum[pl.ds(o * own_heads + g, slots, stride=heads), :] for g in range(own_heads)
        ]
        mls = [part_ml[pl.ds(o * own_heads + g, slots, stride=heads), :] for g in range(own_heads)]
        return jnp.concatenate(sums, 0), jnp.concatenate(mls, 0)

    def joined(one, other):
        (sum_a, ml_a), (sum_b, ml_b) = one, other
        top_a, top_b = ml_a[:, 0:1], ml_b[:, 0:1]
        top = jnp.maximum(top_a, top_b)
        f_a, f_b = jnp.exp(top_a - top), jnp.exp(top_b - top)
        lane = lax.broadcasted_iota(jnp.int32, ml_a.shape, 1)
        total = ml_a * f_a + ml_b * f_b
        return sum_a * f_a + sum_b * f_b, jnp.where(lane < half, top, total)

    def read(buf, k):
        return buf[k, 0:count, :], buf[k, count : 2 * count, :]

    def put(buf, k, value):
        buf[k, 0:count, :] = value[0]
        buf[k, count : 2 * count, :] = value[1]

    put(s_up, 0, own_part(lax.rem(me + h - 1, n)))
    hop(s_up, 0, s_send.at[0], s_recv.at[0], up).start()
    put(s_dn, 0, own_part(lax.rem(me + n - h, n)))
    hop(s_dn, 0, s_send.at[1], s_recv.at[1], down).start()

    def soft_step(k):
        arrival(s_up, k, s_send.at[0], s_recv.at[0], up).wait_recv()
        put(s_up, k, joined(read(s_up, k), own_part(lax.rem(me + h - 1 - k, n))))

        @pl.when(k < h - 1)
        def _():
            hop(s_up, k, s_send.at[0], s_recv.at[0], up).start()

        arrival(s_dn, k, s_send.at[1], s_recv.at[1], down).wait_recv()
        put(s_dn, k, joined(read(s_dn, k), own_part(lax.rem(me + n - h + k, n))))
        hop(s_dn, k, s_send.at[1], s_recv.at[1], down).start()

    def both(k, carry):
        state_step(k, False)
        soft_step(k - early + 1)
        return carry

    lax.fori_loop(early, h, both, 0)

    behind = header_up(h, me)
    for p in range(prompts):
        own = term(p, me, behind[p : p + 1])
        wait_sum(0, r_up, h, p, up)
        wait_sum(1, r_dn, h, p, down)
        handed[0, p] = r_up[h, p] + r_dn[h, p] + own
    state_pair = remote(
        handed.at[0], handed.at[1], pair_send.at[1], pair_recv.at[1], {"batch": 1 - core}
    )
    state_pair.start()

    lax.fori_loop(h - early + 1, h, lambda k, c: (soft_step(k), c)[1], 0)
    state_pair.wait()

    rates_here = rates[:, columns(me)]
    inner = inner_ref[...].astype(jnp.float32)
    gate = gate_ref[...].astype(jnp.float32)
    gated = gate / (1.0 + jnp.exp(-gate))
    driven = step_size_ref[...] * inner
    skipped = skip_ref[...] * inner
    for r in range(slots):
        fresh, _, place = slot_facts(r)
        begin = jnp.where(fresh, handed[lax.div(place, prompts), lax.rem(place, prompts)], res_state_ref[r])
        following = (
            jnp.exp(-rates_here * step_size_ref[r : r + 1, :]) * begin
            + driven[r : r + 1, :] * sin_ref[:, r : r + 1]
        )
        next_ref[r] = following
        readout = jnp.sum(sout_ref[:, r : r + 1] * following, axis=0, keepdims=True)
        mamba_ref[r : r + 1, :] = (readout + skipped[r : r + 1, :]) * gated[r : r + 1, :]

    arrival(s_dn, h, s_send.at[1], s_recv.at[1], down).wait_recv()
    sums, mls = joined(read(s_up, h - 1), read(s_dn, h))
    att_ref[...] = sums / mls[:, half : half + 1]

    def sent(buf, first, last, send, recv, to):
        part = buf.at[pl.ds(first, last - first)]
        remote(part, part, send, recv, {"seq": to}).wait_send()

    sent(t_up, 0, h - 1, t_send.at[0], t_recv.at[0, 0], up)
    sent(t_dn, 0, h, t_send.at[1], t_recv.at[1, 0], down)
    sent(h_up, 0, h, h_send.at[0], h_recv.at[0, 0], up)
    sent(h_dn, 0, h - 1, h_send.at[1], h_recv.at[1, 0], down)
    sent(r_up, 1, h, r_send.at[0], r_recv.at[0, 0, 0], up)
    sent(r_dn, 0, h, r_send.at[1], r_recv.at[1, 0, 0], down)
    sent(s_up, 0, h - 1, s_send.at[0], s_recv.at[0, 0], up)
    sent(s_dn, 0, h, s_send.at[1], s_recv.at[1, 0], down)


def local(
    n,
    prompt_cache,
    prompt_states,
    block_steps,
    prompt_lengths,
    target_slots,
    cache_lengths,
    resident_cache,
    token_cache,
    queries,
    resident_states,
    decay_rates,
    step_sizes,
    inner_input,
    inner_gate,
    state_input,
    state_readout,
    skip_gain,
):
    prompts, block_len, kv_heads, kv_width = prompt_cache.shape
    slots, heads, head_dim = queries.shape
    state, channels = decay_rates.shape
    share = channels // n
    h = n // 2
    own_heads = heads // n
    count = own_heads * slots
    f32, bf16 = jnp.float32, jnp.bfloat16
    smem = pl.BlockSpec(memory_space=pltpu.SMEM)
    vmem = pl.BlockSpec(memory_space=pltpu.VMEM)
    hbm = pl.BlockSpec(memory_space=pltpu.HBM)
    dma, vm = pltpu.SemaphoreType.DMA, pltpu.VMEM
    merged, attention, next_states, mamba_output = pl.pallas_call(
        functools.partial(kernel, n, min(STEPS_BEFORE_ATTENTION, h)),
        out_shape=(
            jax.ShapeDtypeStruct((slots, block_len, kv_heads, kv_width), bf16),
            jax.ShapeDtypeStruct((count, head_dim), f32),
            jax.ShapeDtypeStruct((slots, state, share), f32),
            jax.ShapeDtypeStruct((slots, share), f32),
        ),
        in_specs=[smem] * 3 + [vmem] * 2 + [hbm] + [vmem] * 11,
        out_specs=(vmem, vmem, vmem, vmem),
        scratch_shapes=[
            vm((prompts, state, channels), f32),
            vm((prompts, channels), f32),
            vm((2 * prompts, block_len, kv_heads, kv_width), bf16),
            vm((h + 1, 2 * prompts, share), f32),
            vm((h + 1, 2 * prompts, share), f32),
            vm((h + 1, 2 * prompts, share), f32),
            vm((h + 1, 2 * prompts, share), f32),
            vm((h + 1, prompts, state, share), f32),
            vm((h + 1, prompts, state, share), f32),
            vm((h + 1, 2 * count, head_dim), f32),
            vm((h + 1, 2 * count, head_dim), f32),
            vm((slots * heads, head_dim), f32),
            vm((slots * heads, head_dim), f32),
            vm((2, prompts, state, share), f32),
            dma,
            dma,
            dma,
            dma((2,)),
            dma((2,)),
            dma((2,)),
            dma((2, h + 1)),
            dma((2,)),
            dma((2, h + 1)),
            dma((2,)),
            dma((2, h + 1, prompts)),
            dma((2,)),
            dma((2, h + 1)),
        ],
        compiler_params=pltpu.CompilerParams(
            collective_id=0, has_side_effects=True, vmem_limit_bytes=48 * 1024 * 1024
        ),
    )(
        prompt_lengths,
        target_slots,
        cache_lengths,
        prompt_cache,
        block_steps[:, 0],
        prompt_states[:, 0],
        decay_rates,
        resident_cache[:, :, 0],
        token_cache,
        queries,
        resident_states,
        step_sizes,
        inner_input,
        inner_gate,
        state_input.T,
        state_readout.T,
        skip_gain[None],
    )
    attention = attention.reshape(own_heads, slots, head_dim).transpose(1, 0, 2).astype(bf16)
    return merged[:, :, None], attention, next_states, mamba_output.astype(bf16)


def solution(mesh):
    n = mesh.shape["seq"]
    rows = ("groups", "batch")
    return jax.shard_map(
        functools.partial(local, n),
        mesh=mesh,
        in_specs=(
            P(rows, "seq", None, None),
            P(rows, "seq", None, None),
            P(rows, "seq", None),
            P("groups"),
            P("groups"),
            P(rows),
            P(rows, None, "seq", None, None),
            P(rows, None, None),
            P(rows, None, None),
            P(rows, None, "seq"),
            P(),
            P(rows, "seq"),
            P(rows, "seq"),
            P(rows, "seq"),
            P(rows, None),
            P(rows, None),
            P("seq"),
        ),
        out_specs=(
            P(rows, None, "seq", None, None),
            P(rows, "seq", None),
            P(rows, None, "seq"),
            P(rows, "seq"),
        ),
        check_vma=False,
    )
```

time: 424 us -> 191 us (0.45)
  waiting for transfers between devices: 252 us -> 0 us
  Pallas kernels: 0 us -> 170 us
  other arithmetic: 60.1 us -> 0.6 us
  starting transfers between devices: 57 us -> 0 us
  blocking collectives: 20.9 us -> 0 us
  between operations: 14.1 us -> 0.67 us
    pallas_call x0 -> x1, Pallas kernels: none -> 170 us  [local(): pl.pallas_call(functools.partial(kernel, n, min(STEPS_BEFORE_ATTENTION, h...]
    all_to_all x4 -> x0, waiting for transfers between devices: 134 us -> none  [the longest x1 67.7 us: local(): lax.all_to_all(to_cyclic(prompt_cache, seq_count), 'seq', split_axis=2, c...]
    all_gather x2 -> x0, waiting for transfers between devices: 79.9 us -> none  [the longest x1 79.8 us: carried_in(): everything = lax.all_gather(shard, axis)]
    all_to_all x4 -> x0, starting transfers between devices: 56.8 us -> none  [the longest x1 33.2 us: local(): lax.all_to_all(to_cyclic(prompt_cache, seq_count), 'seq', split_axis=2, c...]
    select_n x35 -> x0, other arithmetic: 45.5 us -> none  [the longest x32 41.8 us: step(): return jnp.where(reached, new, before)]
    reduce_scatter x1 -> x0, waiting for transfers between devices: 38.6 us -> none  [local(): lax.psum_scatter(decay_term(prompt_states[:, 0], behind, usable, decay_ra...]
    all_to_all x1 -> x0, blocking collectives: 20.9 us -> none  [sent_to_all(): lax.all_to_all(jnp.broadcast_to(shard[None], (count, *shard.shape)), axis...]
    mul x3 -> x0, other arithmetic: 7.39 us -> none  [the longest x1 4.86 us: decay_term(): usable[:, None, None] * jnp.exp(-rates[None] * behind[:, None, :]) * states]
  transfers between devices with their start and end apart: 7 -> 0, of which waited for: 6 -> 0; matrix products, arithmetic and copies ran while one was open for 16% -> 0% of each run, Pallas kernels for 0% -> 0%
where the time goes in v1:
time: 191 us; the launch traced here: 187 us
  Pallas kernels  170 us (89%)
  local copies, waits for them, and re-layouts  15.8 us (8%)
    pallas_call x1, Pallas kernels, local(): pl.pallas_call(functools.partial(kernel, n, min(STEPS_BEFORE_ATTENTION, h...  170 us
    unnamed x31, local copies, waits for them, and re-layouts  15.2 us

profile of v1, /device:TPU:37, one launch (start us, length us, event | category | flops | bytes accessed | tf_op | source)
XLA Modules:
  0.0 187.4 jit_solution(17110206165644110345)
XLA Ops:
  0.6 0.8 copy.21
  1.4 0.8 copy.22
  2.1 1.1 copy.28
  3.3 0.0 copy-start
  3.3 1.2 copy-done
  4.5 0.0 copy-start.1
  4.5 1.2 copy-done.1
  5.7 0.0 copy-start.2
  5.7 1.0 copy-done.2
  6.8 0.0 copy-start.3
  6.8 0.9 copy-done.3
  7.7 0.0 copy-start.4
  7.7 0.9 copy-done.4
  8.6 0.0 copy-start.5
  8.6 0.8 copy-done.5
  9.4 0.0 copy-start.6
  9.4 0.7 copy-done.6
  10.1 0.0 copy-start.7
  10.1 0.7 copy-done.7
  10.8 0.0 copy-start.8
  10.8 0.7 copy-done.8
  11.5 0.0 copy-start.9
  11.5 0.7 copy-done.9
  12.2 0.0 copy-start.10
  12.2 0.7 copy-done.10
  12.8 0.7 copy-done.11
  13.5 0.7 copy-done.12
  14.1 170.3 %shard_map.192 = (bf16[8,32,8,256]{3,2,1,0:T(8,128)(2,1)S(1)}, f32[16,128]{1,0:T(8,128)S(1)}, f32[8,16,512]{2,1,0:T(8,128)S(1)}, f32[8,512]{1,0:T(8,128)S(1)}) custom-call(s32[8]{0:T(128)S(1)} %copy-done.10, s32[8]{0:T(128)S(1)} %copy-done.11, s32[8]{0:T(128)S(1)} %copy-done.12, bf16[4,32,8,256]{3,2,1,0:T(8,128)(2,1)S(1)} %copy-done.2, ...), custom_call_target="tpu_custom_call" | custom-call | tf_op jit(solution)/shard_map/pallas_call | solution.py:441
  184.5 0.6 copy.29
  185.1 0.6 convert_element_type.15
  185.7 1.0 copy.32
  186.7 0.7 copy.33
  (3 shorter events, 0.0 us)
Async XLA Ops:
  3.3 1.2 copy-start
  4.5 1.2 copy-start.1
  5.7 1.0 copy-start.2
  6.8 0.9 copy-start.3
  7.7 0.9 copy-start.4
  8.6 0.8 copy-start.5
  9.4 0.7 copy-start.6
  10.1 0.7 copy-start.7
  10.8 0.7 copy-start.8
  11.5 0.7 copy-start.9
  12.2 0.7 copy-start.10
  12.8 0.7 copy-start.11
  13.5 0.7 copy-start.12

commit v2 on v1

v2 whole, which is shorter than its diff:
```python
import functools
import math

import jax
import jax.numpy as jnp
from jax import lax
from jax.experimental import pallas as pl
from jax.experimental.pallas import tpu as pltpu
from jax.sharding import PartitionSpec as P

MESH = pl.DeviceIdType.MESH
STEPS_BEFORE_ATTENTION = 2
PIECE = 2
LANES = 128
LEVELS = 32767.0


def kernel(
    n,
    early,
    plen_hbm,
    target_hbm,
    clen_hbm,
    cache_hbm,
    steps_hbm,
    states_hbm,
    rates_hbm,
    resident_hbm,
    token_hbm,
    query_hbm,
    res_state_hbm,
    step_size_hbm,
    inner_hbm,
    gate_hbm,
    sin_hbm,
    sout_hbm,
    skip_hbm,
    merged_hbm,
    att_ref,
    next_ref,
    mamba_ref,
    plen_ref,
    target_ref,
    clen_ref,
    cache_ref,
    steps_ref,
    rates,
    resident,
    token_ref,
    query_ref,
    res_state_ref,
    step_size_ref,
    inner_ref,
    gate_ref,
    sin_ref,
    sout_ref,
    skip_ref,
    merged,
    states,
    msteps,
    arrived,
    t_up,
    t_dn,
    h_up,
    h_dn,
    r_up,
    r_dn,
    q_up,
    q_dn,
    s_up,
    s_dn,
    part_sum,
    part_ml,
    handed,
    att_all,
    load_sem,
    go_sem,
    states_sem,
    out_sem,
    cache_send,
    cache_recv,
    pair_send,
    pair_recv,
    t_send,
    t_recv,
    h_send,
    h_recv,
    r_send,
    r_recv,
    q_send,
    q_recv,
    s_send,
    s_recv,
):
    h = n // 2
    lead = 1
    me = lax.axis_index("seq")
    core = lax.axis_index("batch")
    up = lax.rem(me + 1, n)
    down = lax.rem(me + n - 1, n)
    own, block_len, kv_heads, kv_width = cache_ref.shape
    prompts = states.shape[0]
    state = states.shape[1]
    share = handed.shape[2]
    slots, heads, head_dim = query_ref.shape
    rows = block_len * kv_heads
    own_heads = heads // n
    group = heads // kv_heads
    mine = pl.ds(core * own, own)

    pairs = (
        (plen_hbm, plen_ref),
        (steps_hbm, steps_ref.at[mine]),
        (cache_hbm, cache_ref),
        (rates_hbm, rates),
        (target_hbm, target_ref),
        (clen_hbm, clen_ref),
        (resident_hbm, resident),
        (token_hbm, token_ref),
        (query_hbm, query_ref),
        (res_state_hbm, res_state_ref),
        (step_size_hbm, step_size_ref),
        (inner_hbm, inner_ref),
        (gate_hbm, gate_ref),
        (sin_hbm, sin_ref),
        (sout_hbm, sout_ref),
        (skip_hbm, skip_ref),
    )
    loads = [
        pltpu.make_async_copy(source, held, load_sem.at[i])
        for i, (source, held) in enumerate(pairs)
    ]
    barrier = pltpu.get_barrier_semaphore()
    for neighbour in (up, down):
        pl.semaphore_signal(barrier, inc=1, device_id={"seq": neighbour}, device_id_type=MESH)
    pl.semaphore_signal(barrier, inc=1, device_id={"batch": 1 - core}, device_id_type=MESH)
    for load in loads:
        load.start()

    def columns(o):
        return pl.ds(pl.multiple_of(o * share, share), share)

    def remote(src, dst, send, recv, where):
        return pltpu.make_async_remote_copy(
            src_ref=src,
            dst_ref=dst,
            send_sem=send,
            recv_sem=recv,
            device_id=where,
            device_id_type=MESH,
        )

    def to_pair(src, dst, i):
        return remote(src, dst, pair_send.at[i], pair_recv.at[i], {"batch": 1 - core})

    def hop(buf, k, send, recv, to):
        return remote(buf.at[k], buf.at[k + 1], send, recv.at[k + 1], {"seq": to})

    def arrival(buf, k, send, recv, to):
        return remote(buf.at[k], buf.at[k], send, recv.at[k], {"seq": to})

    def send_cache(k):
        to = lax.rem(me + k, n)
        remote(
            cache_ref.at[:, to], arrived.at[mine, me], cache_send, cache_recv, {"seq": to}
        ).start()

    for load in loads[:3]:
        load.wait()
    for p in range(own):
        arrived[core * own + p, me] = cache_ref[p, me]

    theirs = pl.ds((1 - lead) * own, own)
    steps_pair = to_pair(steps_ref.at[theirs], steps_ref.at[theirs], 0)
    states_pair = to_pair(states_hbm, states.at[theirs], 1)
    states_load = pltpu.make_async_copy(states_hbm, states.at[pl.ds(lead * own, own)], states_sem)

    pl.semaphore_wait(barrier, 3)

    @pl.when(core != lead)
    def _():
        steps_pair.start()
        states_pair.start()

        def both_ways(k, carry):
            pl.semaphore_wait(go_sem, 1)
            send_cache(k)
            send_cache(n - k)
            return carry

        lax.fori_loop(1, h, both_ways, 0)
        pl.semaphore_wait(go_sem, 1)
        send_cache(h)
        steps_pair.wait_send()
        states_pair.wait_send()

    usable = []
    for p in range(prompts):
        reached = me * block_len < plen_ref[p]
        usable.append(jnp.where(reached, 1.0, 0.0).astype(jnp.float32))

    def parts_of(s):
        own_steps = msteps[:, columns(lax.rem(s + n - h, n))]
        high = jnp.where(me > s, 1.0, 0.0).astype(jnp.float32)
        return high * own_steps, (1.0 - high) * own_steps

    def first_steps(buf, s):
        above, below = parts_of(s)
        buf[0, 0:prompts, :] = above
        buf[0, prompts : 2 * prompts, :] = below

    def more_steps(buf, k, s):
        above, below = parts_of(s)
        buf[k, 0:prompts, :] += above
        buf[k, prompts : 2 * prompts, :] += below

    def let_pair_send():
        pl.semaphore_signal(go_sem, inc=1, device_id={"batch": 1 - core}, device_id_type=MESH)

    def step_ring(k, carry):
        arrival(t_up, k, t_send.at[0], t_recv.at[0], up).wait_recv()
        more_steps(t_up, k, lax.rem(me + h - 1 - k, n))

        @pl.when(k < h - 1)
        def _():
            hop(t_up, k, t_send.at[0], t_recv.at[0], up).start()

        arrival(t_dn, k, t_send.at[1], t_recv.at[1], down).wait_recv()
        more_steps(t_dn, k, lax.rem(me + n - h + k, n))
        hop(t_dn, k, t_send.at[1], t_recv.at[1], down).start()
        let_pair_send()
        send_cache(k)
        send_cache(n - k)
        return carry

    def term(p, o, behind):
        return (
            usable[p]
            * jnp.exp(-rates[:, columns(o)] * behind)
            * states[p, :, columns(o)]
        )

    def coded(buf, tops, k, p, value):
        top = jnp.maximum(jnp.max(jnp.abs(value), keepdims=True), 1e-30)
        buf[k, p] = jnp.floor(value * (LEVELS / top) + 0.5).astype(jnp.int32).astype(jnp.int16)
        tops[k, p // PIECE, p % PIECE : p % PIECE + 1, :] = jnp.broadcast_to(top, (1, LANES))

    def plain(buf, tops, k, p):
        top = tops[k, p // PIECE, p % PIECE : p % PIECE + 1, 0:1]
        return buf[k, p].astype(jnp.int32).astype(jnp.float32) * (top * (1.0 / LEVELS))

    def send_sum(way, buf, tops, k, c, to):
        piece = pl.ds(c * PIECE, PIECE)
        remote(
            tops.at[k, c], tops.at[k + 1, c], q_send.at[way], q_recv.at[way, k + 1, c], {"seq": to}
        ).start()
        remote(
            buf.at[k, piece],
            buf.at[k + 1, piece],
            r_send.at[way],
            r_recv.at[way, k + 1, c],
            {"seq": to},
        ).start()

    def wait_sum(way, buf, tops, k, c, to):
        remote(
            tops.at[k, c], tops.at[k, c], q_send.at[way], q_recv.at[way, k, c], {"seq": to}
        ).wait_recv()
        piece = buf.at[k, pl.ds(c * PIECE, PIECE)]
        remote(piece, piece, r_send.at[way], r_recv.at[way, k, c], {"seq": to}).wait_recv()

    def header_up(k, o):
        arrival(h_up, k, h_send.at[0], h_recv.at[0], up).wait_recv()
        before = jnp.where(me == 0, h_up[k, prompts : 2 * prompts, :], h_up[k, 0:prompts, :])
        return before - msteps[:, columns(o)]

    def state_step(k, first):
        o_up = lax.rem(me + 2 * n - h - k, n)
        o_dn = lax.rem(me + n - h + k, n)
        behind_up = header_up(k, o_up)
        h_up[k, 0:prompts, :] = behind_up
        hop(h_up, k, h_send.at[0], h_recv.at[0], up).start()
        arrival(h_dn, k, h_send.at[1], h_recv.at[1], down).wait_recv()
        behind_dn = jnp.where(me == n - 1, 0.0, h_dn[k])
        h_dn[k] = behind_dn + msteps[:, columns(o_dn)]

        @pl.when(k < h - 1)
        def _():
            hop(h_dn, k, h_send.at[1], h_recv.at[1], down).start()

        for c in range(prompts // PIECE):
            inside = range(c * PIECE, c * PIECE + PIECE)
            up_terms = [term(p, o_up, behind_up[p : p + 1]) for p in inside]
            dn_terms = [term(p, o_dn, behind_dn[p : p + 1]) for p in inside]
            if not first:
                wait_sum(0, r_up, q_up, k, c, up)
            for p, value in zip(inside, up_terms):
                coded(r_up, q_up, k, p, value if first else plain(r_up, q_up, k, p) + value)
            send_sum(0, r_up, q_up, k, c, up)
            wait_sum(1, r_dn, q_dn, k, c, down)
            for p, value in zip(inside, dn_terms):
                coded(r_dn, q_dn, k, p, plain(r_dn, q_dn, k, p) + value)
            send_sum(1, r_dn, q_dn, k, c, down)

    @pl.when(core == lead)
    def _():
        states_load.start()
        steps_pair.wait_recv()
        for p in range(prompts):
            msteps[p : p + 1, :] = steps_ref[p] * usable[p]
        first_steps(t_up, lax.rem(me + h - 1, n))
        hop(t_up, 0, t_send.at[0], t_recv.at[0], up).start()
        first_steps(t_dn, lax.rem(me + n - h, n))
        hop(t_dn, 0, t_send.at[1], t_recv.at[1], down).start()
        lax.fori_loop(1, h, step_ring, 0)
        arrival(t_dn, h, t_send.at[1], t_recv.at[1], down).wait_recv()
        let_pair_send()
        later = t_up[h - 1, 0:prompts, :] + t_dn[h, 0:prompts, :]
        everything = (
            later + t_up[h - 1, prompts : 2 * prompts, :] + t_dn[h, prompts : 2 * prompts, :]
        )
        start = lax.rem(me + n - h, n)
        h_up[0, 0:prompts, :] = later
        h_up[0, prompts : 2 * prompts, :] = everything
        hop(h_up, 0, h_send.at[0], h_recv.at[0], up).start()
        h_dn[0] = later + msteps[:, columns(start)]
        hop(h_dn, 0, h_send.at[1], h_recv.at[1], down).start()
        send_cache(h)
        loads[3].wait()
        states_load.wait()
        states_pair.wait_recv()
        for c in range(prompts // PIECE):
            for p in range(c * PIECE, c * PIECE + PIECE):
                coded(r_dn, q_dn, 0, p, term(p, start, later[p : p + 1]))
            send_sum(1, r_dn, q_dn, 0, c, down)
        state_step(1, True)
        lax.fori_loop(2, early, lambda k, c: (state_step(k, False), c)[1], 0)

    @pl.when(core != lead)
    def _():
        loads[3].wait()

    for load in loads[4:]:
        load.wait()

    remote(
        cache_ref.at[:, pl.ds(0, n - 1)],
        arrived.at[mine, pl.ds(0, n - 1)],
        cache_send,
        cache_recv,
        {"seq": up},
    ).wait()
    cache_pair = to_pair(arrived.at[mine], arrived.at[mine], 2)
    cache_pair.start()
    cache_pair.wait()

    def slot_facts(r):
        slot = core * slots + r
        fresh, length, place = jnp.int32(0), clen_ref[r], jnp.int32(0)
        for p in range(prompts):
            hit = target_ref[p] == slot
            fresh = jnp.where(hit, 1, fresh)
            length = jnp.where(hit, plen_ref[p], length)
            place = jnp.where(hit, p, place)
        return fresh == 1, length, place

    def attend(r, carry):
        fresh, length, place = slot_facts(r)
        chosen = jnp.where(
            fresh, arrived[place].astype(jnp.float32), resident[r].astype(jnp.float32)
        )
        position = lax.broadcasted_iota(jnp.int32, chosen.shape, 0) * n + me
        chosen = jnp.where(position < length, chosen, 0.0)
        token = jnp.broadcast_to(token_ref[r].astype(jnp.float32)[None], chosen.shape)
        chosen = jnp.where(position == length, token, chosen)
        merged[r] = chosen.astype(jnp.bfloat16)
        flat = chosen.reshape(rows, kv_width).astype(jnp.bfloat16)
        score = lax.dot_general(
            query_ref[r],
            flat[:, :head_dim],
            (((1,), (1,)), ((), ())),
            preferred_element_type=jnp.float32,
        ) * (1.0 / math.sqrt(head_dim))
        column = lax.broadcasted_iota(jnp.int32, score.shape, 1)
        row = lax.broadcasted_iota(jnp.int32, score.shape, 0)
        seen = (lax.rem(column, kv_heads) == lax.div(row, group)) & (
            lax.div(column, kv_heads) * n + me <= length
        )
        score = jnp.where(seen, score, -1e30)
        top = jnp.max(score, axis=1, keepdims=True)
        weight = jnp.where(seen, jnp.exp(score - top), 0.0)
        total = jnp.sum(weight, axis=1, keepdims=True)
        summed = jnp.dot(
            weight.astype(jnp.bfloat16), flat[:, head_dim:], preferred_element_type=jnp.float32
        )
        at = pl.ds(pl.multiple_of((core * slots + r) * heads, heads), heads)
        part_sum[at, :] = summed
        lane = lax.broadcasted_iota(jnp.int32, summed.shape, 1)
        part_ml[at, :] = jnp.where(lane < head_dim // 2, top, total)
        return carry

    lax.fori_loop(0, slots, attend, 0)
    write = pltpu.make_async_copy(merged, merged_hbm, out_sem)
    write.start()
    there = pl.ds((1 - lead) * slots * heads, slots * heads)
    sum_pair = to_pair(part_sum.at[there], part_sum.at[there], 3)
    ml_pair = to_pair(part_ml.at[there], part_ml.at[there], 4)
    handed_pair = to_pair(handed, handed, 5)
    att_pair = to_pair(att_all.at[:, pl.ds((1 - lead) * slots, slots)], att_ref, 6)

    @pl.when(core != lead)
    def _():
        sum_pair.start()
        ml_pair.start()
        sum_pair.wait_send()
        ml_pair.wait_send()

    count = own_heads * 2 * slots
    half = head_dim // 2

    def own_part(o):
        at = [pl.ds(o * own_heads + g, 2 * slots, stride=heads) for g in range(own_heads)]
        return (
            jnp.concatenate([part_sum[i, :] for i in at], 0),
            jnp.concatenate([part_ml[i, :] for i in at], 0),
        )

    def joined(one, other):
        (sum_a, ml_a), (sum_b, ml_b) = one, other
        top_a, top_b = ml_a[:, 0:1], ml_b[:, 0:1]
        top = jnp.maximum(top_a, top_b)
        f_a, f_b = jnp.exp(top_a - top), jnp.exp(top_b - top)
        lane = lax.broadcasted_iota(jnp.int32, ml_a.shape, 1)
        total = ml_a * f_a + ml_b * f_b
        return sum_a * f_a + sum_b * f_b, jnp.where(lane < half, top, total)

    def read(buf, k):
        return buf[k, 0:count, :], buf[k, count : 2 * count, :]

    def put(buf, k, value):
        buf[k, 0:count, :] = value[0]
        buf[k, count : 2 * count, :] = value[1]

    def soft_step(k):
        arrival(s_up, k, s_send.at[0], s_recv.at[0], up).wait_recv()
        put(s_up, k, joined(read(s_up, k), own_part(lax.rem(me + h - 1 - k, n))))

        @pl.when(k < h - 1)
        def _():
            hop(s_up, k, s_send.at[0], s_recv.at[0], up).start()

        arrival(s_dn, k, s_send.at[1], s_recv.at[1], down).wait_recv()
        put(s_dn, k, joined(read(s_dn, k), own_part(lax.rem(me + n - h + k, n))))
        hop(s_dn, k, s_send.at[1], s_recv.at[1], down).start()

    def both(k, carry):
        state_step(k, False)
        soft_step(k - early + 1)
        return carry

    @pl.when(core == lead)
    def _():
        sum_pair.wait_recv()
        ml_pair.wait_recv()
        put(s_up, 0, own_part(lax.rem(me + h - 1, n)))
        hop(s_up, 0, s_send.at[0], s_recv.at[0], up).start()
        put(s_dn, 0, own_part(lax.rem(me + n - h, n)))
        hop(s_dn, 0, s_send.at[1], s_recv.at[1], down).start()
        lax.fori_loop(early, h, both, 0)

        behind = header_up(h, me)
        for c in range(prompts // PIECE):
            inside = range(c * PIECE, c * PIECE + PIECE)
            own_terms = [term(p, me, behind[p : p + 1]) for p in inside]
            wait_sum(0, r_up, q_up, h, c, up)
            wait_sum(1, r_dn, q_dn, h, c, down)
            for p, value in zip(inside, own_terms):
                handed[p] = plain(r_up, q_up, h, p) + plain(r_dn, q_dn, h, p) + value
        handed_pair.start()
        lax.fori_loop(h - early + 1, h, lambda k, c: (soft_step(k), c)[1], 0)
        arrival(s_dn, h, s_send.at[1], s_recv.at[1], down).wait_recv()
        sums, mls = joined(read(s_up, h - 1), read(s_dn, h))
        att = sums / mls[:, half : half + 1]
        for g in range(own_heads):
            att_all[g] = att[g * 2 * slots : (g + 1) * 2 * slots]
            att_ref[g] = att[g * 2 * slots + lead * slots : g * 2 * slots + (lead + 1) * slots]
        att_pair.start()

    @pl.when(core != lead)
    def _():
        handed_pair.wait_recv()

    rates_here = rates[:, columns(me)]
    inner = inner_ref[...].astype(jnp.float32)
    gate = gate_ref[...].astype(jnp.float32)
    gated = gate / (1.0 + jnp.exp(-gate))
    driven = step_size_ref[...] * inner
    skipped = skip_ref[...] * inner

    def upright(row):
        square = (state, state)
        same = lax.broadcasted_iota(jnp.int32, square, 0) == lax.broadcasted_iota(
            jnp.int32, square, 1
        )
        return jnp.sum(jnp.where(same, jnp.broadcast_to(row, square), 0.0), axis=1, keepdims=True)

    for r in range(slots):
        fresh, _, place = slot_facts(r)
        begin = jnp.where(fresh, handed[place], res_state_ref[r])
        following = (
            jnp.exp(-rates_here * step_size_ref[r : r + 1, :]) * begin
            + driven[r : r + 1, :] * upright(sin_ref[r : r + 1, :])
        )
        next_ref[r] = following
        readout = jnp.sum(upright(sout_ref[r : r + 1, :]) * following, axis=0, keepdims=True)
        mamba_ref[r : r + 1, :] = (readout + skipped[r : r + 1, :]) * gated[r : r + 1, :]

    def sent(buf, first, last, send, recv, to):
        part = buf.at[pl.ds(first, last - first)]
        remote(part, part, send, recv, {"seq": to}).wait_send()

    @pl.when(core == lead)
    def _():
        sent(t_up, 0, h - 1, t_send.at[0], t_recv.at[0, 0], up)
        sent(t_dn, 0, h, t_send.at[1], t_recv.at[1, 0], down)
        sent(h_up, 0, h, h_send.at[0], h_recv.at[0, 0], up)
        sent(h_dn, 0, h - 1, h_send.at[1], h_recv.at[1, 0], down)
        sent(r_up, 1, h, r_send.at[0], r_recv.at[0, 0, 0], up)
        sent(r_dn, 0, h, r_send.at[1], r_recv.at[1, 0, 0], down)
        sent(q_up, 1, h, q_send.at[0], q_recv.at[0, 0, 0], up)
        sent(q_dn, 0, h, q_send.at[1], q_recv.at[1, 0, 0], down)
        sent(s_up, 0, h - 1, s_send.at[0], s_recv.at[0, 0], up)
        sent(s_dn, 0, h, s_send.at[1], s_recv.at[1, 0], down)
        handed_pair.wait_send()
        att_pair.wait_send()

    @pl.when(core != lead)
    def _():
        att_pair.wait_recv()

    write.wait()


def local(
    n,
    prompt_cache,
    prompt_states,
    block_steps,
    prompt_lengths,
    target_slots,
    cache_lengths,
    resident_cache,
    token_cache,
    queries,
    resident_states,
    decay_rates,
    step_sizes,
    inner_input,
    inner_gate,
    state_input,
    state_readout,
    skip_gain,
):
    own, block_len, kv_heads, kv_width = prompt_cache.shape
    prompts = prompt_lengths.shape[0]
    slots, heads, head_dim = queries.shape
    state, channels = decay_rates.shape
    share = channels // n
    h = n // 2
    own_heads = heads // n
    count = own_heads * 2 * slots
    f32, bf16 = jnp.float32, jnp.bfloat16
    vmem = pl.BlockSpec(memory_space=pltpu.VMEM)
    hbm = pl.BlockSpec(memory_space=pltpu.HBM)
    dma, vm = pltpu.SemaphoreType.DMA, pltpu.VMEM
    merged, attention, next_states, mamba_output = pl.pallas_call(
        functools.partial(kernel, n, min(STEPS_BEFORE_ATTENTION, h)),
        out_shape=(
            jax.ShapeDtypeStruct((slots, block_len, kv_heads, kv_width), bf16),
            jax.ShapeDtypeStruct((own_heads, slots, head_dim), f32),
            jax.ShapeDtypeStruct((slots, state, share), f32),
            jax.ShapeDtypeStruct((slots, share), f32),
        ),
        in_specs=[hbm] * 17,
        out_specs=(hbm, vmem, vmem, vmem),
        scratch_shapes=[
            pltpu.SMEM(prompt_lengths.shape, jnp.int32),
            pltpu.SMEM(target_slots.shape, jnp.int32),
            pltpu.SMEM(cache_lengths.shape, jnp.int32),
            vm(prompt_cache.shape, bf16),
            vm((prompts, 1, channels), f32),
            vm(decay_rates.shape, f32),
            vm((slots, block_len, kv_heads, kv_width), bf16),
            vm(token_cache.shape, bf16),
            vm(queries.shape, bf16),
            vm(resident_states.shape, f32),
            vm(step_sizes.shape, f32),
            vm(inner_input.shape, bf16),
            vm(inner_gate.shape, bf16),
            vm(state_input.shape, f32),
            vm(state_readout.shape, f32),
            vm((1, share), f32),
            vm((slots, block_len, kv_heads, kv_width), bf16),
            vm((prompts, state, channels), f32),
            vm((prompts, channels), f32),
            vm((prompts, block_len, kv_heads, kv_width), bf16),
            vm((h + 1, 2 * prompts, share), f32),
            vm((h + 1, 2 * prompts, share), f32),
            vm((h + 1, 2 * prompts, share), f32),
            vm((h + 1, prompts, share), f32),
            vm((h + 1, prompts, state, share), jnp.int16),
            vm((h + 1, prompts, state, share), jnp.int16),
            vm((h + 1, prompts // PIECE, 8, LANES), f32),
            vm((h + 1, prompts // PIECE, 8, LANES), f32),
            vm((h + 1, 2 * count, head_dim), f32),
            vm((h + 1, 2 * count, head_dim), f32),
            vm((2 * slots * heads, head_dim), f32),
            vm((2 * slots * heads, head_dim), f32),
            vm((prompts, state, share), f32),
            vm((own_heads, 2 * slots, head_dim), f32),
            dma((16,)),
            pltpu.SemaphoreType.REGULAR,
            dma,
            dma,
            dma,
            dma,
            dma((7,)),
            dma((7,)),
            dma((2,)),
            dma((2, h + 1)),
            dma((2,)),
            dma((2, h + 1)),
            dma((2,)),
            dma((2, h + 1, prompts // PIECE)),
            dma((2,)),
            dma((2, h + 1, prompts // PIECE)),
            dma((2,)),
            dma((2, h + 1)),
        ],
        compiler_params=pltpu.CompilerParams(
            collective_id=0, has_side_effects=True, vmem_limit_bytes=62 * 1024 * 1024
        ),
    )(
        prompt_lengths,
        target_slots,
        cache_lengths,
        prompt_cache,
        block_steps,
        prompt_states[:, 0],
        decay_rates,
        resident_cache[:, :, 0],
        token_cache,
        queries,
        resident_states,
        step_sizes,
        inner_input,
        inner_gate,
        state_input,
        state_readout,
        skip_gain[None],
    )
    attention = attention.transpose(1, 0, 2).astype(bf16)
    return merged[:, :, None], attention, next_states, mamba_output.astype(bf16)


def solution(mesh):
    n = mesh.shape["seq"]
    rows = ("groups", "batch")
    return jax.shard_map(
        functools.partial(local, n),
        mesh=mesh,
        in_specs=(
            P(rows, "seq", None, None),
            P(rows, "seq", None, None),
            P(rows, "seq", None),
            P("groups"),
            P("groups"),
            P(rows),
            P(rows, None, "seq", None, None),
            P(rows, None, None),
            P(rows, None, None),
            P(rows, None, "seq"),
            P(),
            P(rows, "seq"),
            P(rows, "seq"),
            P(rows, "seq"),
            P(rows, None),
            P(rows, None),
            P("seq"),
        ),
        out_specs=(
            P(rows, None, "seq", None, None),
            P(rows, "seq", None),
            P(rows, None, "seq"),
            P(rows, "seq"),
        ),
        check_vma=False,
    )
```

time: 191 us -> 165 us (0.86); the launches traced: 187 us -> 164 us
  Pallas kernels: 170 us -> 156 us
  local copies, waits for them, and re-layouts: 15.8 us -> 4.53 us
    pallas_call x1, Pallas kernels: 170 us -> 156 us  [local(): pl.pallas_call(functools.partial(kernel, n, min(STEPS_BEFORE_ATTENTION, h...]
    unnamed x31 -> x3, local copies, waits for them, and re-layouts: 15.2 us -> 4.53 us
where the time goes in v2:
time: 165 us; the launch traced here: 164 us
  Pallas kernels  156 us (95%)
  local copies, waits for them, and re-layouts  4.53 us (3%)
  other arithmetic  2.02 us (1%)
    pallas_call x1, Pallas kernels, local(): pl.pallas_call(functools.partial(kernel, n, min(STEPS_BEFORE_ATTENTION, h...  156 us
    unnamed x3, local copies, waits for them, and re-layouts  4.53 us

profile of v2, /device:TPU:37, one launch (start us, length us, event | category | flops | bytes accessed | tf_op | source)
XLA Modules:
  0.0 163.6 jit_solution(10958776215142447328)
XLA Ops:
  0.6 156.4 %shard_map.192 = (bf16[8,32,8,256]{3,2,1,0:T(8,128)(2,1)}, f32[2,8,128]{2,1,0:T(8,128)}, f32[8,16,512]{2,1,0:T(8,128)}, f32[8,512]{1,0:T(8,128)}) custom-call(s32[8]{0:T(128)} %plen_hbm.1, s32[8]{0:T(128)} %target_hbm.1, s32[8]{0:T(128)} %clen_hbm.1, bf16[4,32,8,256]{3,2,1,0:T(8,128)(2,1)} %cache_hbm.1, f32[4,1,16384]{2,1,0:T(1,128)} %steps_hbm.1, ...), custom_call_target="tpu_custom_call" | custom-call | tf_op jit(solution)/shard_map/pallas_call | solution.py:576
  157.0 0.7 convert_bitcast_fusion
  157.7 0.6 copy.22
  158.3 1.3 convert_element_type.11
  159.7 2.3 %copy.25 = bf16[8,32,1,8,256]{4,3,2,1,0:T(8,128)(2,1)} copy(bf16[8,32,1,8,256]{4,3,2,1,0:T(8,128)(2,1)} %bitcast.9) | data formatting | bytes 2097152
  161.9 1.7 %copy.26 = f32[8,16,512]{2,1,0:T(8,128)} copy(f32[8,16,512]{2,1,0:T(8,128)} %get-tuple-element.22) | data formatting | bytes 524288

commit v3 on v2

--- a/solution.py
+++ b/solution.py
@@ -9,7 +9,7 @@
 from jax.sharding import PartitionSpec as P
 
 MESH = pl.DeviceIdType.MESH
-STEPS_BEFORE_ATTENTION = 2
+STEPS_BEFORE_ATTENTION = 9
 PIECE = 2
 LANES = 128
 LEVELS = 32767.0
@@ -59,6 +59,8 @@
     states,
     msteps,
     arrived,
+    c_up,
+    c_dn,
     t_up,
     t_dn,
     h_up,
@@ -67,18 +69,19 @@
     r_dn,
     q_up,
     q_dn,
-    s_up,
-    s_dn,
+    soft_out,
+    facts_out,
+    soft_in,
+    facts_in,
     part_sum,
     part_ml,
     handed,
-    att_all,
     load_sem,
-    go_sem,
     states_sem,
     out_sem,
     cache_send,
     cache_recv,
+    c_recv,
     pair_send,
     pair_recv,
     t_send,
@@ -98,7 +101,7 @@
     core = lax.axis_index("batch")
     up = lax.rem(me + 1, n)
     down = lax.rem(me + n - 1, n)
-    own, block_len, kv_heads, kv_width = cache_ref.shape
+    own, block_len, kv_heads, kv_width = cache_hbm.shape
     prompts = states.shape[0]
     state = states.shape[1]
     share = handed.shape[2]
@@ -111,7 +114,7 @@
     pairs = (
         (plen_hbm, plen_ref),
         (steps_hbm, steps_ref.at[mine]),
-        (cache_hbm, cache_ref),
+        (cache_hbm, cache_ref.at[mine]),
         (rates_hbm, rates),
         (target_hbm, target_ref),
         (clen_hbm, clen_ref),
@@ -159,20 +162,57 @@
     def arrival(buf, k, send, recv, to):
         return remote(buf.at[k], buf.at[k], send, recv.at[k], {"seq": to})
 
-    def send_cache(k):
-        to = lax.rem(me + k, n)
-        remote(
-            cache_ref.at[:, to], arrived.at[mine, me], cache_send, cache_recv, {"seq": to}
-        ).start()
+    side = h + 1
+
+    def cache_hop(way, src, k, j):
+        buf = c_up if way == 0 else c_dn
+        to = up if way == 0 else down
+        origin = lax.rem(me + (1 - k if way == 0 else k - 1) + n, n)
+
+        @pl.when(j == k)
+        def _():
+            remote(src, arrived.at[:, origin], cache_send, cache_recv, {"seq": to}).start()
+
+        @pl.when(j > k)
+        def _():
+            at = k * side + j
+            remote(src, buf.at[at], cache_send, c_recv.at[way, at], {"seq": to}).start()
+
+    def cache_first(i, carry):
+        j = h - i
+        cache_hop(0, cache_ref.at[:, lax.rem(me + j, n)], 1, j)
+
+        @pl.when(j < h)
+        def _():
+            cache_hop(1, cache_ref.at[:, lax.rem(me + n - j, n)], 1, j)
+
+        return carry
+
+    def cache_phase(k, carry):
+        def block(i, inner):
+            j = h - i
+            at = (k - 1) * side + j
+            remote(c_up.at[at], c_up.at[at], cache_send, c_recv.at[0, at], {"seq": up}).wait_recv()
+            cache_hop(0, c_up.at[at], k, j)
+
+            @pl.when(j < h)
+            def _():
+                remote(
+                    c_dn.at[at], c_dn.at[at], cache_send, c_recv.at[1, at], {"seq": down}
+                ).wait_recv()
+                cache_hop(1, c_dn.at[at], k, j)
+
+            return inner
+
+        return lax.fori_loop(0, h + 1 - k, block, carry)
 
     for load in loads[:3]:
         load.wait()
-    for p in range(own):
-        arrived[core * own + p, me] = cache_ref[p, me]
-
     theirs = pl.ds((1 - lead) * own, own)
     steps_pair = to_pair(steps_ref.at[theirs], steps_ref.at[theirs], 0)
     states_pair = to_pair(states_hbm, states.at[theirs], 1)
+    lead_half = pl.ds(lead * own, own)
+    lead_cache = to_pair(cache_hbm, cache_ref.at[lead_half], 2)
     states_load = pltpu.make_async_copy(states_hbm, states.at[pl.ds(lead * own, own)], states_sem)
 
     pl.semaphore_wait(barrier, 3)
@@ -181,16 +221,12 @@
     def _():
         steps_pair.start()
         states_pair.start()
-
-        def both_ways(k, carry):
-            pl.semaphore_wait(go_sem, 1)
-            send_cache(k)
-            send_cache(n - k)
-            return carry
-
-        lax.fori_loop(1, h, both_ways, 0)
-        pl.semaphore_wait(go_sem, 1)
-        send_cache(h)
+        lead_cache.wait_recv()
+        for p in range(prompts):
+            arrived[p, me] = cache_ref[p, me]
+
+        lax.fori_loop(0, h, cache_first, 0)
+        lax.fori_loop(2, h + 1, cache_phase, 0)
         steps_pair.wait_send()
         states_pair.wait_send()
 
@@ -214,9 +250,6 @@
         buf[k, 0:prompts, :] += above
         buf[k, prompts : 2 * prompts, :] += below
 
-    def let_pair_send():
-        pl.semaphore_signal(go_sem, inc=1, device_id={"batch": 1 - core}, device_id_type=MESH)
-
     def step_ring(k, carry):
         arrival(t_up, k, t_send.at[0], t_recv.at[0], up).wait_recv()
         more_steps(t_up, k, lax.rem(me + h - 1 - k, n))
@@ -228,9 +261,6 @@
         arrival(t_dn, k, t_send.at[1], t_recv.at[1], down).wait_recv()
         more_steps(t_dn, k, lax.rem(me + n - h + k, n))
         hop(t_dn, k, t_send.at[1], t_recv.at[1], down).start()
-        let_pair_send()
-        send_cache(k)
-        send_cache(n - k)
         return carry
 
     def term(p, o, behind):
@@ -304,6 +334,7 @@
 
     @pl.when(core == lead)
     def _():
+        lead_cache.start()
         states_load.start()
         steps_pair.wait_recv()
         for p in range(prompts):
@@ -314,7 +345,6 @@
         hop(t_dn, 0, t_send.at[1], t_recv.at[1], down).start()
         lax.fori_loop(1, h, step_ring, 0)
         arrival(t_dn, h, t_send.at[1], t_recv.at[1], down).wait_recv()
-        let_pair_send()
         later = t_up[h - 1, 0:prompts, :] + t_dn[h, 0:prompts, :]
         everything = (
             later + t_up[h - 1, prompts : 2 * prompts, :] + t_dn[h, prompts : 2 * prompts, :]
@@ -325,7 +355,6 @@
         hop(h_up, 0, h_send.at[0], h_recv.at[0], up).start()
         h_dn[0] = later + msteps[:, columns(start)]
         hop(h_dn, 0, h_send.at[1], h_recv.at[1], down).start()
-        send_cache(h)
         loads[3].wait()
         states_load.wait()
         states_pair.wait_recv()
@@ -343,16 +372,21 @@
     for load in loads[4:]:
         load.wait()
 
-    remote(
-        cache_ref.at[:, pl.ds(0, n - 1)],
-        arrived.at[mine, pl.ds(0, n - 1)],
-        cache_send,
-        cache_recv,
-        {"seq": up},
-    ).wait()
-    cache_pair = to_pair(arrived.at[mine], arrived.at[mine], 2)
-    cache_pair.start()
-    cache_pair.wait()
+    cache_pair = to_pair(arrived, arrived, 4)
+
+    @pl.when(core != lead)
+    def _():
+        some = arrived.at[:, pl.ds(0, n - 1)]
+        remote(some, some, cache_send, cache_recv, {"seq": up}).wait_recv()
+        cache_pair.start()
+        moved = c_up.at[pl.ds(0, h * h)]
+        remote(moved, moved, cache_send, cache_recv, {"seq": up}).wait_send()
+        cache_pair.wait_send()
+
+    @pl.when(core == lead)
+    def _():
+        lead_cache.wait_send()
+        cache_pair.wait_recv()
 
     def slot_facts(r):
         slot = core * slots + r
@@ -393,80 +427,49 @@
         summed = jnp.dot(
             weight.astype(jnp.bfloat16), flat[:, head_dim:], preferred_element_type=jnp.float32
         )
-        at = pl.ds(pl.multiple_of((core * slots + r) * heads, heads), heads)
-        part_sum[at, :] = summed
+        at = pl.ds(pl.multiple_of(r * heads, heads), heads)
+        most = jnp.maximum(jnp.max(jnp.abs(summed), axis=1, keepdims=True), 1e-30)
+        part_sum[at, :] = jnp.floor(summed * (LEVELS / most) + 0.5)
         lane = lax.broadcasted_iota(jnp.int32, summed.shape, 1)
-        part_ml[at, :] = jnp.where(lane < head_dim // 2, top, total)
+        part_ml[at, :] = jnp.where(
+            lane < count, top, jnp.where(lane < 2 * count, total, most * (1.0 / LEVELS))
+        )
         return carry
 
+    count = own_heads * slots
     lax.fori_loop(0, slots, attend, 0)
     write = pltpu.make_async_copy(merged, merged_hbm, out_sem)
     write.start()
-    there = pl.ds((1 - lead) * slots * heads, slots * heads)
-    sum_pair = to_pair(part_sum.at[there], part_sum.at[there], 3)
-    ml_pair = to_pair(part_ml.at[there], part_ml.at[there], 4)
-    handed_pair = to_pair(handed, handed, 5)
-    att_pair = to_pair(att_all.at[:, pl.ds((1 - lead) * slots, slots)], att_ref, 6)
-
-    @pl.when(core != lead)
-    def _():
-        sum_pair.start()
-        ml_pair.start()
-        sum_pair.wait_send()
-        ml_pair.wait_send()
-
-    count = own_heads * 2 * slots
-    half = head_dim // 2
-
-    def own_part(o):
-        at = [pl.ds(o * own_heads + g, 2 * slots, stride=heads) for g in range(own_heads)]
-        return (
-            jnp.concatenate([part_sum[i, :] for i in at], 0),
-            jnp.concatenate([part_ml[i, :] for i in at], 0),
-        )
-
-    def joined(one, other):
-        (sum_a, ml_a), (sum_b, ml_b) = one, other
-        top_a, top_b = ml_a[:, 0:1], ml_b[:, 0:1]
-        top = jnp.maximum(top_a, top_b)
-        f_a, f_b = jnp.exp(top_a - top), jnp.exp(top_b - top)
-        lane = lax.broadcasted_iota(jnp.int32, ml_a.shape, 1)
-        total = ml_a * f_a + ml_b * f_b
-        return sum_a * f_a + sum_b * f_b, jnp.where(lane < half, top, total)
-
-    def read(buf, k):
-        return buf[k, 0:count, :], buf[k, count : 2 * count, :]
-
-    def put(buf, k, value):
-        buf[k, 0:count, :] = value[0]
-        buf[k, count : 2 * count, :] = value[1]
-
-    def soft_step(k):
-        arrival(s_up, k, s_send.at[0], s_recv.at[0], up).wait_recv()
-        put(s_up, k, joined(read(s_up, k), own_part(lax.rem(me + h - 1 - k, n))))
-
-        @pl.when(k < h - 1)
-        def _():
-            hop(s_up, k, s_send.at[0], s_recv.at[0], up).start()
-
-        arrival(s_dn, k, s_send.at[1], s_recv.at[1], down).wait_recv()
-        put(s_dn, k, joined(read(s_dn, k), own_part(lax.rem(me + n - h + k, n))))
-        hop(s_dn, k, s_send.at[1], s_recv.at[1], down).start()
-
-    def both(k, carry):
-        state_step(k, False)
-        soft_step(k - early + 1)
+    handed_pair = to_pair(handed, handed, 3)
+
+    tall = lax.broadcasted_iota(jnp.int32, (count, LANES), 0)
+    wide = lax.broadcasted_iota(jnp.int32, (count, LANES), 1)
+
+    def pack(o):
+        at = [pl.ds(o * own_heads + g, slots, stride=heads) for g in range(own_heads)]
+        coarse = jnp.concatenate([part_sum[i, :] for i in at], 0)
+        facts = jnp.concatenate([part_ml[i, :] for i in at], 0)
+        flat = jnp.sum(jnp.where(lax.rem(wide, count) == tall, facts, 0.0), axis=0, keepdims=True)
+        return coarse.astype(jnp.int32).astype(jnp.int16), flat
+
+    def send_part(k, carry):
+        to = lax.rem(me + k, n)
+        soft_out[to], facts_out[to] = pack(to)
+        remote(soft_out.at[to], soft_in.at[me], s_send.at[0], s_recv.at[0], {"seq": to}).start()
+        remote(facts_out.at[to], facts_in.at[me], s_send.at[1], s_recv.at[1], {"seq": to}).start()
         return carry
+
+    def both_parts(k, carry):
+        send_part(h - k, carry)
+        return send_part(h + k, carry)
+
+    send_part(h, 0)
+    lax.fori_loop(1, h, both_parts, 0)
+    soft_in[me], facts_in[me] = pack(me)
 
     @pl.when(core == lead)
     def _():
-        sum_pair.wait_recv()
-        ml_pair.wait_recv()
-        put(s_up, 0, own_part(lax.rem(me + h - 1, n)))
-        hop(s_up, 0, s_send.at[0], s_recv.at[0], up).start()
-        put(s_dn, 0, own_part(lax.rem(me + n - h, n)))
-        hop(s_dn, 0, s_send.at[1], s_recv.at[1], down).start()
-        lax.fori_loop(early, h, both, 0)
+        lax.fori_loop(early, h, lambda k, c: (state_step(k, False), c)[1], 0)
 
         behind = header_up(h, me)
         for c in range(prompts // PIECE):
@@ -477,14 +480,6 @@
             for p, value in zip(inside, own_terms):
                 handed[p] = plain(r_up, q_up, h, p) + plain(r_dn, q_dn, h, p) + value
         handed_pair.start()
-        lax.fori_loop(h - early + 1, h, lambda k, c: (soft_step(k), c)[1], 0)
-        arrival(s_dn, h, s_send.at[1], s_recv.at[1], down).wait_recv()
-        sums, mls = joined(read(s_up, h - 1), read(s_dn, h))
-        att = sums / mls[:, half : half + 1]
-        for g in range(own_heads):
-            att_all[g] = att[g * 2 * slots : (g + 1) * 2 * slots]
-            att_ref[g] = att[g * 2 * slots + lead * slots : g * 2 * slots + (lead + 1) * slots]
-        att_pair.start()
 
     @pl.when(core != lead)
     def _():
@@ -514,6 +509,24 @@
         next_ref[r] = following
         readout = jnp.sum(upright(sout_ref[r : r + 1, :]) * following, axis=0, keepdims=True)
         mamba_ref[r : r + 1, :] = (readout + skipped[r : r + 1, :]) * gated[r : r + 1, :]
+
+    for buf, i in ((soft_in, 0), (facts_in, 1)):
+        most_of = buf.at[pl.ds(0, n - 1)]
+        remote(most_of, most_of, s_send.at[i], s_recv.at[i], {"seq": up}).wait()
+    facts = facts_in[:, 0, :]
+    within = lax.broadcasted_iota(jnp.int32, facts.shape, 1) < count
+    tops = jnp.where(within, facts, 0.0)
+    totals = jnp.where(within, pltpu.roll(facts, LANES - count, 1), 0.0)
+    scales = jnp.where(within, pltpu.roll(facts, LANES - 2 * count, 1), 0.0)
+    factors = jnp.exp(tops - jnp.max(tops, axis=0, keepdims=True))
+    whole = jnp.sum(totals * factors, axis=0, keepdims=True)
+    scales = scales * factors / jnp.where(whole > 0.0, whole, 1.0)
+    gathered = jnp.zeros((count, head_dim), jnp.float32)
+    for j in range(n):
+        row = jnp.broadcast_to(scales[j : j + 1, :], (count, LANES))
+        factor = jnp.sum(jnp.where(wide == tall, row, 0.0), axis=1, keepdims=True)
+        gathered = gathered + factor * soft_in[j].astype(jnp.int32).astype(jnp.float32)
+    att_ref[...] = gathered
 
     def sent(buf, first, last, send, recv, to):
         part = buf.at[pl.ds(first, last - first)]
@@ -529,14 +542,7 @@
         sent(r_dn, 0, h, r_send.at[1], r_recv.at[1, 0, 0], down)
         sent(q_up, 1, h, q_send.at[0], q_recv.at[0, 0, 0], up)
         sent(q_dn, 0, h, q_send.at[1], q_recv.at[1, 0, 0], down)
-        sent(s_up, 0, h - 1, s_send.at[0], s_recv.at[0, 0], up)
-        sent(s_dn, 0, h, s_send.at[1], s_recv.at[1, 0], down)
         handed_pair.wait_send()
-        att_pair.wait_send()
-
-    @pl.when(core != lead)
-    def _():
-        att_pair.wait_recv()
 
     write.wait()
 
@@ -568,7 +574,7 @@
     share = channels // n
     h = n // 2
     own_heads = heads // n
-    count = own_heads * 2 * slots
+    count = own_heads * slots
     f32, bf16 = jnp.float32, jnp.bfloat16
     vmem = pl.BlockSpec(memory_space=pltpu.VMEM)
     hbm = pl.BlockSpec(memory_space=pltpu.HBM)
@@ -577,7 +583,7 @@
         functools.partial(kernel, n, min(STEPS_BEFORE_ATTENTION, h)),
         out_shape=(
             jax.ShapeDtypeStruct((slots, block_len, kv_heads, kv_width), bf16),
-            jax.ShapeDtypeStruct((own_heads, slots, head_dim), f32),
+            jax.ShapeDtypeStruct((count, head_dim), f32),
             jax.ShapeDtypeStruct((slots, state, share), f32),
             jax.ShapeDtypeStruct((slots, share), f32),
         ),
@@ -587,7 +593,7 @@
             pltpu.SMEM(prompt_lengths.shape, jnp.int32),
             pltpu.SMEM(target_slots.shape, jnp.int32),
             pltpu.SMEM(cache_lengths.shape, jnp.int32),
-            vm(prompt_cache.shape, bf16),
+            vm((prompts, block_len, kv_heads, kv_width), bf16),
             vm((prompts, 1, channels), f32),
             vm(decay_rates.shape, f32),
             vm((slots, block_len, kv_heads, kv_width), bf16),
@@ -604,6 +610,8 @@
             vm((prompts, state, channels), f32),
             vm((prompts, channels), f32),
             vm((prompts, block_len, kv_heads, kv_width), bf16),
+            vm(((h + 1) * (h + 1), prompts, kv_heads, kv_width), bf16),
+            vm(((h + 1) * (h + 1), prompts, kv_heads, kv_width), bf16),
             vm((h + 1, 2 * prompts, share), f32),
             vm((h + 1, 2 * prompts, share), f32),
             vm((h + 1, 2 * prompts, share), f32),
@@ -612,20 +620,21 @@
             vm((h + 1, prompts, state, share), jnp.int16),
             vm((h + 1, prompts // PIECE, 8, LANES), f32),
             vm((h + 1, prompts // PIECE, 8, LANES), f32),
-            vm((h + 1, 2 * count, head_dim), f32),
-            vm((h + 1, 2 * count, head_dim), f32),
-            vm((2 * slots * heads, head_dim), f32),
-            vm((2 * slots * heads, head_dim), f32),
+            vm((n, count, head_dim), jnp.int16),
+            vm((n, 1, LANES), f32),
+            vm((n, count, head_dim), jnp.int16),
+            vm((n, 1, LANES), f32),
+            vm((slots * heads, head_dim), f32),
+            vm((slots * heads, head_dim), f32),
             vm((prompts, state, share), f32),
-            vm((own_heads, 2 * slots, head_dim), f32),
             dma((16,)),
-            pltpu.SemaphoreType.REGULAR,
             dma,
             dma,
             dma,
             dma,
-            dma((7,)),
-            dma((7,)),
+            dma((2, (h + 1) * (h + 1))),
+            dma((5,)),
+            dma((5,)),
             dma((2,)),
             dma((2, h + 1)),
             dma((2,)),
@@ -635,7 +644,7 @@
             dma((2,)),
             dma((2, h + 1, prompts // PIECE)),
             dma((2,)),
-            dma((2, h + 1)),
+            dma((2,)),
         ],
         compiler_params=pltpu.CompilerParams(
             collective_id=0, has_side_effects=True, vmem_limit_bytes=62 * 1024 * 1024
@@ -659,7 +668,7 @@
         state_readout,
         skip_gain[None],
     )
-    attention = attention.transpose(1, 0, 2).astype(bf16)
+    attention = attention.reshape(own_heads, slots, head_dim).transpose(1, 0, 2).astype(bf16)
     return merged[:, :, None], attention, next_states, mamba_output.astype(bf16)
 
 

time: 165 us -> 152 us (0.921)
  Pallas kernels: 156 us -> 145 us
    pallas_call x1, Pallas kernels: 156 us -> 145 us  [local(): pl.pallas_call(functools.partial(kernel, n, min(STEPS_BEFORE_ATTENTION, h...]
    unnamed x3 -> x2, local copies, waits for them, and re-layouts: 4.53 us -> 3.93 us
where the time goes in v3:
time: 152 us
  Pallas kernels  145 us (95%)
  local copies, waits for them, and re-layouts  4.53 us (3%)
  other arithmetic  2.02 us (1%)
    pallas_call x1, Pallas kernels, local(): pl.pallas_call(functools.partial(kernel, n, min(STEPS_BEFORE_ATTENTION, h...  145 us
    unnamed x2, local copies, waits for them, and re-layouts  3.93 us

profile of v3, /device:TPU:37, one launch (start us, length us, event | category | flops | bytes accessed | tf_op | source)
XLA Modules:
  0.0 152.0 jit_solution(10496470573108472894)
XLA Ops:
  0.6 144.8 %shard_map.192 = (bf16[8,32,8,256]{3,2,1,0:T(8,128)(2,1)}, f32[16,128]{1,0:T(8,128)}, f32[8,16,512]{2,1,0:T(8,128)}, f32[8,512]{1,0:T(8,128)}) custom-call(s32[8]{0:T(128)} %plen_hbm.1, s32[8]{0:T(128)} %target_hbm.1, s32[8]{0:T(128)} %clen_hbm.1, bf16[4,32,8,256]{3,2,1,0:T(8,128)(2,1)} %cache_hbm.1, f32[4,1,16384]{2,1,0:T(1,128)} %steps_hbm.1, ...), custom_call_target="tpu_custom_call" | custom-call | tf_op jit(solution)/shard_map/pallas_call | solution.py:582
  145.4 0.7 convert_bitcast_fusion
  146.1 0.6 copy.24
  146.7 1.3 convert_element_type.15
  148.1 2.3 %copy.27 = bf16[8,32,1,8,256]{4,3,2,1,0:T(8,128)(2,1)} copy(bf16[8,32,1,8,256]{4,3,2,1,0:T(8,128)(2,1)} %bitcast.12) | data formatting | bytes 2097152
  150.3 1.7 %copy.28 = f32[8,16,512]{2,1,0:T(8,128)} copy(f32[8,16,512]{2,1,0:T(8,128)} %get-tuple-element.22) | data formatting | bytes 524288

commit v4 on v3

--- a/solution.py
+++ b/solution.py
@@ -9,7 +9,7 @@
 from jax.sharding import PartitionSpec as P
 
 MESH = pl.DeviceIdType.MESH
-STEPS_BEFORE_ATTENTION = 9
+STEPS_BEFORE_ATTENTION = 12
 PIECE = 2
 LANES = 128
 LEVELS = 32767.0

time: 152 us -> 156 us (1.026)
  Pallas kernels: 145 us -> 148 us
    pallas_call x1, Pallas kernels: 145 us -> 148 us  [local(): pl.pallas_call(functools.partial(kernel, n, min(STEPS_BEFORE_ATTENTION, h...]
where the time goes in v4:
time: 156 us; the launch traced here: 155 us
  Pallas kernels  148 us (95%)
  local copies, waits for them, and re-layouts  4.53 us (3%)
  other arithmetic  2.02 us (1%)
    pallas_call x1, Pallas kernels, local(): pl.pallas_call(functools.partial(kernel, n, min(STEPS_BEFORE_ATTENTION, h...  148 us
    unnamed x2, local copies, waits for them, and re-layouts  3.93 us

profile of v4, /device:TPU:37, one launch (start us, length us, event | category | flops | bytes accessed | tf_op | source)
XLA Modules:
  0.0 155.4 jit_solution(11638119195830876521)
XLA Ops:
  0.6 148.2 %shard_map.192 = (bf16[8,32,8,256]{3,2,1,0:T(8,128)(2,1)}, f32[16,128]{1,0:T(8,128)}, f32[8,16,512]{2,1,0:T(8,128)}, f32[8,512]{1,0:T(8,128)}) custom-call(s32[8]{0:T(128)} %plen_hbm.1, s32[8]{0:T(128)} %target_hbm.1, s32[8]{0:T(128)} %clen_hbm.1, bf16[4,32,8,256]{3,2,1,0:T(8,128)(2,1)} %cache_hbm.1, f32[4,1,16384]{2,1,0:T(1,128)} %steps_hbm.1, ...), custom_call_target="tpu_custom_call" | custom-call | tf_op jit(solution)/shard_map/pallas_call | solution.py:582
  148.9 0.7 convert_bitcast_fusion
  149.6 0.6 copy.24
  150.2 1.3 convert_element_type.15
  151.5 2.3 %copy.27 = bf16[8,32,1,8,256]{4,3,2,1,0:T(8,128)(2,1)} copy(bf16[8,32,1,8,256]{4,3,2,1,0:T(8,128)(2,1)} %bitcast.12) | data formatting | bytes 2097152
  153.8 1.7 %copy.28 = f32[8,16,512]{2,1,0:T(8,128)} copy(f32[8,16,512]{2,1,0:T(8,128)} %get-tuple-element.22) | data formatting | bytes 524288
